TPU v7x, 256 devices: a whole 4x4x8 slice. The times are simulated.
256 devices in a mesh: grp: 4 (over z_hi), ep: 32 (over y, x, z_lo), tp: 2 (over core).
Axes of the slice: x: 4, y: 4, z: 8 (z_hi: 4, z_lo: 2; z = z_hi * 2 + z_lo), core: 2. Of those that a mesh axis runs over, the one named last changes fastest.
Arguments:
- tokens: bfloat16 [1024, 7168], P('ep', 'tp'), may hold values from -6 to 6
- gates: float32 [1024, 8], P('ep'), may hold values from 0.05 to 1
- expert_ids: int32 [1024, 8], P('ep'), may hold values from 0 to 31, all different within a row; in each aligned block of 16 rows (0 to 15, 16 to 31, ...) at most 8 rows name the same one
- gate_weight: bfloat16 [32, 7168, 2048], P('ep', None, ('grp', 'tp')), may hold values from -0.0625 to 0.0625
- up_weight: bfloat16 [32, 7168, 2048], P('ep', None, ('grp', 'tp')), may hold values from -0.0625 to 0.0625
- down_weight: bfloat16 [32, 2048, 7168], P('ep', ('grp', 'tp')), may hold values from -0.125 to 0.125
Outputs:
- mixed_out: bfloat16 [1024, 7168], P('ep', ('grp', 'tp'))
Inputs may be any that keep to these rules, and one draw needn't show every extreme that they name: `expert_ids`: within each aligned block of 16 rows, the 8 experts of a row differ, and no expert is named by more than 8 rows; some expert is named by exactly 8 rows in some blocks.
All inputs are finite; a program needn't handle non-finite values.
Results may differ from a plain program's by a relative error of at most 0.013.
Values may be sent and summed in bfloat16 or wider, within the bound.
No kernel may reach another device: no remote copies, remote signals or barrier semaphores. Data moves between devices by JAX's collectives and lax.ppermute only.
A program may use at most 128 MiB of HBM per device.

v0:
```python
import jax
import jax.numpy as jnp
from jax import lax
from jax.sharding import PartitionSpec as P

TOP = 8
EXPERTS = 32
MB = 2
CAP = 8


def local(tokens, gates, expert_ids, gate_weight, up_weight, down_weight):
    experts_here = gate_weight.shape[0]
    per_micro = tokens.shape[0] // MB
    half_width = tokens.shape[1]
    full_width = down_weight.shape[2]
    sources = lax.axis_size("ep")
    slots = EXPERTS * CAP
    share = full_width // (lax.axis_size("grp") * lax.axis_size("tp"))
    results = []
    for micro in range(MB):
        rows_in = tokens[micro * per_micro : (micro + 1) * per_micro]
        chosen = expert_ids[micro * per_micro : (micro + 1) * per_micro]
        weights = gates[micro * per_micro : (micro + 1) * per_micro]
        flat = chosen.reshape(-1)
        onehot = (flat[:, None] == lax.iota(jnp.int32, EXPERTS)[None, :]).astype(jnp.int32)
        before = jnp.cumsum(onehot, axis=0) - onehot
        slot = jnp.sum(before * onehot, axis=1)
        target = (flat * CAP + slot).reshape(per_micro, TOP)
        match = (target[None, :, :] == lax.iota(jnp.int32, slots)[:, None, None]).astype(
            jnp.float32
        )
        placing = jnp.sum(match, axis=2).astype(jnp.bfloat16)
        mixing = jnp.transpose(jnp.sum(match * weights[None, :, :], axis=2))
        sent = jnp.dot(placing, rows_in, preferred_element_type=jnp.float32).astype(jnp.bfloat16)
        sent = sent.reshape(EXPERTS, CAP, half_width)
        arrived = lax.all_to_all(sent, "ep", split_axis=0, concat_axis=0, tiled=True)
        piece = lax.all_gather(arrived, "tp", axis=2, tiled=True)
        count = piece.shape[2]
        blocked = piece.reshape(sources, experts_here, CAP, count)
        gate_part = jnp.einsum(
            "secd,edh->sech", blocked, gate_weight, preferred_element_type=jnp.float32
        )
        up_part = jnp.einsum(
            "secd,edh->sech", blocked, up_weight, preferred_element_type=jnp.float32
        )
        hidden = (jax.nn.silu(gate_part) * up_part).astype(jnp.bfloat16)
        term = jnp.einsum("sech,ehd->dsec", hidden, down_weight, preferred_element_type=jnp.float32)
        summed = lax.psum_scatter(
            term.reshape(share * lax.axis_size(("grp", "tp")), sources * experts_here * CAP).astype(
                jnp.bfloat16
            ),
            ("grp", "tp"),
            scatter_dimension=0,
            tiled=True,
        )
        returned = lax.all_to_all(summed, "ep", split_axis=1, concat_axis=1, tiled=True)
        mixed = lax.dot_general(
            mixing,
            returned.astype(jnp.float32),
            (((1,), (1,)), ((), ())),
            precision=lax.Precision.HIGHEST,
        )
        results.append(mixed.astype(jnp.bfloat16))
    return jnp.concatenate(results, axis=0)


def solution(mesh):
    placed = (
        P("ep", "tp"),
        P("ep", None),
        P("ep", None),
        P("ep", None, ("grp", "tp")),
        P("ep", None, ("grp", "tp")),
        P("ep", ("grp", "tp"), None),
    )
    return jax.shard_map(
        local, mesh=mesh, in_specs=placed, out_specs=P("ep", ("grp", "tp")), check_vma=False
    )
```

profile of v0, /device:TPU:2, one launch (start us, length us, event | category | flops | bytes accessed | tf_op | source)
XLA Modules:
  0.0 237.2 jit_solution(7277891140350822664)
XLA Ops:
  6.5 0.8 fusion.70
  7.4 0.1 copy.20
  7.4 0.8 fusion.71
  8.3 0.1 copy.27
  8.3 0.1 eq.56
  8.4 0.1 fusion.65
  8.5 0.2 reduce_window_sum.17
  8.7 0.2 select_reduce_fusion.3
  8.9 0.1 reduce_sum.59
  9.0 0.2 convert_reduce_fusion.1
  9.2 2.9 %fusion.2 = bf16[32,8,3584]{2,1,0:T(8,128)(2,1)} fusion(bf16[32,3584]{1,0:T(8,128)(2,1)} %param.6, bf16[256,16]{0,1:T(8,128)(2,1)S(1)} %get-tuple-element.5), kind=kOutput, calls=%fused_computation.6 | convolution fusion | flops 30277632 | bytes 1957888 | tf_op jit(solution)/shard_map/dot_general | solution.py:35
  12.0 9.0 %all-to-all-start = ((bf16[32,8,3584]{2,1,0:T(8,128)(2,1)}), bf16[32,8,3584]{2,1,0:T(8,128)(2,1)S(1)}, u32[]{:S(2)}, u32[]{:S(2)}) async-start(bf16[32,8,3584]{2,1,0:T(8,128)(2,1)} %fusion.2), calls=%async_computation | async-start | bytes 3670016 | tf_op jit(solution)/shard_map/all_to_all | solution.py:37
  21.0 0.0 all-gather.3.cloned.1.call-start
  21.1 0.1 copy.22
  21.1 0.1 copy.28
  21.2 0.1 eq.63
  21.3 0.1 fusion.64
  21.4 0.2 reduce_window_sum.18
  21.6 0.2 select_reduce_fusion.2
  21.7 0.1 reduce_sum.63
  21.8 0.2 convert_reduce_fusion
  22.0 24.4 %all-to-all-done = bf16[32,8,3584]{2,1,0:T(8,128)(2,1)S(1)} async-done(((bf16[32,8,3584]{2,1,0:T(8,128)(2,1)}), bf16[32,8,3584]{2,1,0:T(8,128)(2,1)S(1)}, u32[]{:S(2)}, u32[]{:S(2)}) %all-to-all-start) | async-done | bytes 1835040 | tf_op jit(solution)/shard_map/all_to_all | solution.py:37
  46.4 1.3 copy-done
  47.7 0.0 all-gather.3.cloned.1.call-update
  47.7 0.0 all-gather.5.cloned.1.call-start
  47.8 0.7 fusion.3
  48.4 28.8 %all_to_all.34 = bf16[32,8,3584]{2,1,0:T(8,128)(2,1)} all-to-all(bf16[32,8,3584]{2,1,0:T(8,128)(2,1)S(1)} %fusion.3), channel_id=1, replica_groups=mesh['grp'=4,'ep'=32,'tp'=2] {'ep'}, dimensions={0} | all-to-all | bytes 3670016 | tf_op jit(solution)/shard_map/all_to_all | solution.py:37
  77.2 0.0 all-gather.5.cloned.1.call-update
  77.3 0.0 reduce-scatter.7.cloned.1.call-start
  77.3 0.0 all-gather.3.cloned.1.call-done
  77.3 4.3 %fusion.14 = f32[32,1,8,256]{3,2,0,1:T(8,128)S(1)} fusion(bf16[32,8,7168]{2,1,0:T(8,128)(2,1)} %all-gather.3.cloned.1.call-done, bf16[1,7168,256]{2,1,0:T(8,128)(2,1)} %param.9), kind=kOutput, calls=%fused_computation.18 | convolution fusion | flops 939524096 | bytes 7602176 | tf_op jit(solution)/shard_map/secd,edh->sech/dot_general | solution.py:41
  81.6 10.1 %fusion = bf16[7168,256]{0,1:T(8,128)(2,1)} fusion(bf16[1,256,7168]{2,1,0:T(8,128)(2,1)} %param.11, bf16[32,8,7168]{2,1,0:T(8,128)(2,1)} %all-gather.3.cloned.1.call-done, bf16[1,7168,256]{2,1,0:T(8,128)(2,1)} %param.10, f32[32,1,8,256]{3,2,0,1:T(8,128)S(1)} %fusion.14), kind=kOutput, calls=%fused_computation.2 | convolution fusion | flops 1881276416 | bytes 14942208 | tf_op jit(solution)/shard_map/sech,ehd->dsec/dot_general | solution.py:48
  91.7 6.2 %copy.23 = bf16[7168,256]{1,0:T(8,128)(2,1)} copy(bf16[7168,256]{0,1:T(8,128)(2,1)} %fusion) | data formatting | bytes 7340032
  97.9 0.2 reduce-scatter.9.cloned.1.call-start
  98.2 0.0 all-gather.5.cloned.1.call-done
  98.2 4.3 %fusion.17 = f32[32,1,8,256]{3,2,0,1:T(8,128)S(1)} fusion(bf16[32,8,7168]{2,1,0:T(8,128)(2,1)} %all-gather.5.cloned.1.call-done, bf16[1,7168,256]{2,1,0:T(8,128)(2,1)} %param.9), kind=kOutput, calls=%fused_computation.19 | convolution fusion | flops 939524096 | bytes 7602176 | tf_op jit(solution)/shard_map/secd,edh->sech/dot_general | solution.py:41
  102.5 10.1 %fusion.1 = bf16[7168,256]{0,1:T(8,128)(2,1)} fusion(bf16[1,256,7168]{2,1,0:T(8,128)(2,1)} %param.11, bf16[32,8,7168]{2,1,0:T(8,128)(2,1)} %all-gather.5.cloned.1.call-done, bf16[1,7168,256]{2,1,0:T(8,128)(2,1)} %param.10, f32[32,1,8,256]{3,2,0,1:T(8,128)S(1)} %fusion.17), kind=kOutput, calls=%fused_computation.3 | convolution fusion | flops 1881276416 | bytes 14942208 | tf_op jit(solution)/shard_map/sech,ehd->dsec/dot_general | solution.py:48
  112.6 5.9 %copy.25 = bf16[7168,256]{1,0:T(8,128)(2,1)} copy(bf16[7168,256]{0,1:T(8,128)(2,1)} %fusion.1) | data formatting | bytes 7340032
  118.5 32.4 %reduce-scatter.7.cloned.1.call-done = bf16[896,256]{1,0:T(8,128)(2,1)} async-done(((bf16[7168,256]{1,0:T(8,128)(2,1)}), bf16[896,256]{1,0:T(8,128)(2,1)}) %reduce-scatter.7.cloned.1.call-update) | async-done | bytes 458768
  150.9 2.0 copy.24
  152.9 9.3 %all-to-all-start.1 = ((bf16[896,32,8]{0,2,1:T(8,128)(2,1)}), bf16[896,32,8]{0,2,1:T(8,128)(2,1)S(1)}, u32[]{:S(2)}, u32[]{:S(2)}) async-start(bf16[896,32,8]{0,2,1:T(8,128)(2,1)} %bitcast.16), calls=%async_computation.1 | async-start | bytes 917504 | tf_op jit(solution)/shard_map/all_to_all | solution.py:57
  162.3 47.4 %reduce-scatter.9.cloned.1.call-done = bf16[896,256]{1,0:T(8,128)(2,1)} async-done(((bf16[7168,256]{1,0:T(8,128)(2,1)}), bf16[896,256]{1,0:T(8,128)(2,1)}) %reduce-scatter.9.cloned.1.call-update) | async-done | bytes 458768
  209.7 2.0 copy.26
  211.7 7.0 %all-to-all-start.3 = ((bf16[896,32,8]{0,2,1:T(8,128)(2,1)}), bf16[896,32,8]{0,2,1:T(8,128)(2,1)S(1)}, u32[]{:S(2)}, u32[]{:S(2)}) async-start(bf16[896,32,8]{0,2,1:T(8,128)(2,1)} %bitcast.29), calls=%async_computation.3 | async-start | bytes 917504 | tf_op jit(solution)/shard_map/all_to_all | solution.py:57
  218.7 0.3 convolution_convert_fusion.5
  219.0 10.8 %all-to-all-done.3 = bf16[896,32,8]{0,2,1:T(8,128)(2,1)S(1)} async-done(((bf16[896,32,8]{0,2,1:T(8,128)(2,1)}), bf16[896,32,8]{0,2,1:T(8,128)(2,1)S(1)}, u32[]{:S(2)}, u32[]{:S(2)}) %all-to-all-start.3) | async-done | bytes 458784 | tf_op jit(solution)/shard_map/all_to_all | solution.py:57
  229.8 0.3 convolution_convert_fusion.4
  230.1 0.6 pad_maximum_fusion
  (8 shorter events, 0.1 us)
Async XLA Ops:
  9.1 38.6 %copy-start.1 = (bf16[32,3584]{1,0:T(8,128)(2,1)S(1)}, bf16[32,3584]{1,0:T(8,128)(2,1)}, u32[]{:S(2)}) copy-start(bf16[32,3584]{1,0:T(8,128)(2,1)} %param.6) | copy-start | bytes 688132
  12.0 34.3 %all-to-all-start = ((bf16[32,8,3584]{2,1,0:T(8,128)(2,1)}), bf16[32,8,3584]{2,1,0:T(8,128)(2,1)S(1)}, u32[]{:S(2)}, u32[]{:S(2)}) async-start(bf16[32,8,3584]{2,1,0:T(8,128)(2,1)} %fusion.2), calls=%async_computation | async-start | bytes 3670016 | tf_op jit(solution)/shard_map/all_to_all | solution.py:37
  21.0 56.3 %all-gather.3.cloned.1.call-start = ((), (), s32[]{:S(2)}) async-start(), calls=%async_computation.6 | async-start | bytes 5505024 | tf_op jit(solution)/shard_map/all_gather | solution.py:38
  46.4 1.3 copy-start
  47.7 50.5 %all-gather.5.cloned.1.call-start = ((), (), s32[]{:S(2)}) async-start(), calls=%async_computation.7 | async-start | bytes 5505024 | tf_op jit(solution)/shard_map/all_gather | solution.py:38
  77.3 73.7 %reduce-scatter.7.cloned.1.call-start = ((), (), s32[]{:S(2)}) async-start(), calls=%async_computation.8 | async-start | bytes 4128768
  97.9 111.8 %reduce-scatter.9.cloned.1.call-start = ((), (), s32[]{:S(2)}) async-start(), calls=%async_computation.9 | async-start | bytes 4128768
  152.9 58.8 %all-to-all-start.1 = ((bf16[896,32,8]{0,2,1:T(8,128)(2,1)}), bf16[896,32,8]{0,2,1:T(8,128)(2,1)S(1)}, u32[]{:S(2)}, u32[]{:S(2)}) async-start(bf16[896,32,8]{0,2,1:T(8,128)(2,1)} %bitcast.16), calls=%async_computation.1 | async-start | bytes 917504 | tf_op jit(solution)/shard_map/all_to_all | solution.py:57
  211.7 18.0 %all-to-all-start.3 = ((bf16[896,32,8]{0,2,1:T(8,128)(2,1)}), bf16[896,32,8]{0,2,1:T(8,128)(2,1)S(1)}, u32[]{:S(2)}, u32[]{:S(2)}) async-start(bf16[896,32,8]{0,2,1:T(8,128)(2,1)} %bitcast.29), calls=%async_computation.3 | async-start | bytes 917504 | tf_op jit(solution)/shard_map/all_to_all | solution.py:57
Sparse Core Ops, SparseCore 0:
  47.8 17.1 all-gather.2
  77.4 17.3 all-gather.4
  98.1 52.8 reduce-scatter.6
  153.4 56.3 reduce-scatter.8
where the time goes:
time: 239 us; the launch traced here: 237 us
  waiting for transfers between devices  115 us (48%)
  matrix products  32.9 us (14%)
  blocking collectives  28.8 us (12%)
  starting transfers between devices  25.6 us (11%)
  local copies, waits for them, and re-layouts  19.7 us (8%)
  between operations  13.3 us (6%)
    unnamed x6, waiting for transfers between devices  79.9 us
    all_to_all x1, blocking collectives, local(): lax.all_to_all(sent, 'ep', split_axis=0, concat_axis=0, tiled=True)  28.8 us
    all_to_all x1, waiting for transfers between devices, local(): lax.all_to_all(sent, 'ep', split_axis=0, concat_axis=0, tiled=True)  24.4 us
    dot_general x2, matrix products, local(): jnp.einsum('sech,ehd->dsec', hidden, down_weight, preferred_element_type=...  20.2 us
    unnamed x10, local copies, waits for them, and re-layouts  17.6 us
    all_to_all x2, starting transfers between devices, local(): lax.all_to_all(summed, 'ep', split_axis=1, concat_axis=1, tiled=True)  16.3 us
    all_to_all x2, waiting for transfers between devices, local(): lax.all_to_all(summed, 'ep', split_axis=1, concat_axis=1, tiled=True)  10.8 us
    all_to_all x1, starting transfers between devices, local(): lax.all_to_all(sent, 'ep', split_axis=0, concat_axis=0, tiled=True)  8.97 us
  transfers between devices with their start and end apart: 7, of which 4 were waited for; matrix products, arithmetic and copies ran while one was open for 20% of the time, Pallas kernels for 0%

commit v1 on v0

v1 whole, which is shorter than its diff:
```python
import jax
import jax.numpy as jnp
from jax import lax
from jax.experimental import pallas as pl
from jax.experimental.pallas import tpu as pltpu
from jax.sharding import PartitionSpec as P

EXPERTS = 32
CAP = 8
MB = 2
INTERPRET = False
BF = jnp.bfloat16
F32 = jnp.float32


def dot(a, b):
    return jnp.dot(a, b, preferred_element_type=F32)


def other_core(a):
    return lax.ppermute(a, "tp", [(0, 1), (1, 0)])


def hidden_body(t, own, peer, gate, up, out, acc):
    step = pl.program_id(0)
    width = gate.shape[1]

    def partial_sums(x):
        g, u = dot(x, gate[...]), dot(x, up[...])

        @pl.when(step == 0)
        def _():
            acc[:, :width] = g
            acc[:, width:] = u

        @pl.when(step > 0)
        def _():
            acc[:, :width] += g
            acc[:, width:] += u

    @pl.when(step < 2)
    def _():
        partial_sums(own[...])

    @pl.when(step >= 2)
    def _():
        partial_sums(peer[...])

    @pl.when(step == 3)
    def _():
        g, u = acc[:, :width], acc[:, width:]
        out[...] = (g * jax.nn.sigmoid(g) * u).astype(BF)


def hidden_of(own, peer, gate, up, t):
    depth, width = gate.shape
    slots = own.shape[0]
    block = depth // 4

    def rows(i, t_ref):
        mine = t_ref[0]
        return jnp.where(i < 2, 2 * mine + i, 2 * (1 - mine) + i - 2), 0

    weight = pl.BlockSpec((block, width), rows)
    return pl.pallas_call(
        hidden_body,
        out_shape=jax.ShapeDtypeStruct((slots, width), BF),
        grid_spec=pltpu.PrefetchScalarGridSpec(
            num_scalar_prefetch=1,
            grid=(4,),
            in_specs=[
                pl.BlockSpec((slots, block), lambda i, t_ref: (0, jnp.minimum(i, 1))),
                pl.BlockSpec((slots, block), lambda i, t_ref: (0, jnp.maximum(i - 2, 0))),
                weight,
                weight,
            ],
            out_specs=pl.BlockSpec((slots, width), lambda i, t_ref: (0, 0)),
            scratch_shapes=[pltpu.VMEM((slots, 2 * width), F32)],
        ),
        interpret=INTERPRET,
        name="hidden",
    )(t, own, peer, gate, up)


def down_body(t, hidden, weight, out):
    out[...] = dot(hidden[...], weight[...]).astype(BF)


def down_add_body(t, hidden, weight, term, out):
    out[...] = (dot(hidden[...], weight[...]) + term[...].astype(F32)).astype(BF)


def down(hidden, weight, which, term=None):
    slots, inner = hidden.shape
    block = weight.shape[1] // 8
    ins = [
        pl.BlockSpec((slots, inner), lambda i, t: (0, 0)),
        pl.BlockSpec((inner, block), lambda i, t: (0, 2 * i + t[0])),
    ]
    piece = pl.BlockSpec((slots, block), lambda i, t: (0, i))
    return pl.pallas_call(
        down_body if term is None else down_add_body,
        out_shape=jax.ShapeDtypeStruct((slots, 4 * block), BF),
        grid_spec=pltpu.PrefetchScalarGridSpec(
            num_scalar_prefetch=1,
            grid=(4,),
            in_specs=ins if term is None else ins + [piece],
            out_specs=piece,
        ),
        interpret=INTERPRET,
        name="down" if term is None else "down_add",
    )(which, hidden, weight, *(() if term is None else (term,)))


def split3(v):
    high = lax.reduce_precision(v, 8, 7)
    middle = lax.reduce_precision(v - high, 8, 7)
    return jnp.concatenate([high, middle, v - high - middle], axis=0).astype(BF)


def local(tokens, gates, expert_ids, gate_weight, up_weight, down_weight):
    gate, up, downw = gate_weight[0], up_weight[0], down_weight[0]
    t = lax.axis_index("tp").astype(jnp.int32).reshape(1)
    count = tokens.shape[0] // MB
    width = tokens.shape[1]
    slots = EXPERTS * CAP
    sent, mixes = [], []
    for m in range(MB):
        part = slice(m * count, (m + 1) * count)
        flat = expert_ids[part].reshape(-1)
        onehot = (flat[:, None] == lax.iota(jnp.int32, EXPERTS)[None, :]).astype(jnp.int32)
        before = jnp.cumsum(onehot, axis=0) - onehot
        slot = jnp.sum(before * onehot, axis=1)
        target = (flat * CAP + slot).reshape(count, -1)
        match = (target[None] == lax.iota(jnp.int32, slots)[:, None, None]).astype(F32)
        placing = jnp.sum(match, axis=2).astype(BF)
        mixes.append(split3(jnp.transpose(jnp.sum(match * gates[part][None], axis=2))))
        sent.append(dot(placing, tokens[part]).astype(BF).reshape(EXPERTS, CAP, width))
    results = []
    for m in range(MB):
        rows = lax.all_to_all(sent[m], "ep", split_axis=0, concat_axis=0, tiled=True)
        rows = rows.reshape(slots, width)
        hidden = hidden_of(rows, other_core(rows), gate, up, t)
        term = other_core(down(hidden, downw, 1 - t))
        out = down(hidden, downw, t, term).reshape(EXPERTS, CAP, width)
        back = lax.all_to_all(out, "ep", split_axis=0, concat_axis=0, tiled=True)
        mixed = dot(mixes[m], back.reshape(slots, width))
        results.append(mixed[:count] + mixed[count : 2 * count] + mixed[2 * count :])
    mixed = jnp.concatenate(results, axis=0).astype(BF)
    blocks = jnp.transpose(mixed.reshape(MB * count, 4, width // 4), (1, 0, 2))
    shares = lax.all_to_all(blocks, "grp", split_axis=0, concat_axis=0, tiled=True)
    return jnp.sum(shares.astype(F32), axis=0).astype(BF)


def solution(mesh):
    placed = (
        P("ep", "tp"),
        P("ep", None),
        P("ep", None),
        P("ep", None, ("grp", "tp")),
        P("ep", None, ("grp", "tp")),
        P("ep", ("grp", "tp"), None),
    )
    return jax.shard_map(
        local, mesh=mesh, in_specs=placed, out_specs=P("ep", ("grp", "tp")), check_vma=False
    )
```

time: 239 us -> 165 us (0.69)
  waiting for transfers between devices: 115 us -> 75.7 us
  Pallas kernels: 0 us -> 31.6 us
  matrix products: 32.9 us -> 7.06 us
  local copies, waits for them, and re-layouts: 19.7 us -> 3.62 us
  between operations: 13.3 us -> 0.17 us
  blocking collectives: 28.8 us -> 16.9 us
    unnamed x6 -> x0, waiting for transfers between devices: 79.9 us -> none
    all_to_all x3 -> x4, waiting for transfers between devices: 35.1 us -> 71.6 us  [the longest x2 40.6 us: local(): lax.all_to_all(sent[m], 'ep', split_axis=0, concat_axis=0, tiled=True)]
    pallas_call x0 -> x6, Pallas kernels: none -> 31.6 us  [the longest x4 17.9 us: down(): pl.pallas_call(down_body if term is None else down_add_body, out_shape=ja...]
    dot_general x8 -> x4, matrix products: 32.9 us -> 7.06 us  [dot(): return jnp.dot(a, b, preferred_element_type=F32)]
    unnamed x10 -> x8, local copies, waits for them, and re-layouts: 17.6 us -> 1.44 us
    all_to_all x1, blocking collectives: 28.8 us -> 16.9 us  [local(): lax.all_to_all(blocks, 'grp', split_axis=0, concat_axis=0, tiled=True)]
    ppermute x0 -> x4, waiting for transfers between devices: none -> 4.13 us  [other_core(): return lax.ppermute(a, 'tp', [(0, 1), (1, 0)])]
    all_to_all x3 -> x4, starting transfers between devices: 25.3 us -> 27.1 us  [the longest x2 14.8 us: local(): lax.all_to_all(sent[m], 'ep', split_axis=0, concat_axis=0, tiled=True)]
  transfers between devices with their start and end apart: 7 -> 8, of which waited for: 4 -> 5; matrix products, arithmetic and copies ran while one was open for 20% -> 2% of each run, Pallas kernels for 0% -> 19%
where the time goes in v1:
time: 165 us; the launch traced here: 164 us
  waiting for transfers between devices  75.7 us (46%)
  Pallas kernels  31.6 us (19%)
  starting transfers between devices  27.3 us (17%)
  blocking collectives  16.9 us (10%)
  matrix products  7.06 us (4%)
  local copies, waits for them, and re-layouts  3.62 us (2%)
  other arithmetic  1.96 us (1%)
    all_to_all x2, waiting for transfers between devices, local(): lax.all_to_all(sent[m], 'ep', split_axis=0, concat_axis=0, tiled=True)  40.6 us
    all_to_all x2, waiting for transfers between devices, local(): back = lax.all_to_all(out, 'ep', split_axis=0, concat_axis=0, tiled=True)  31 us
    pallas_call x4, Pallas kernels, down(): pl.pallas_call(down_body if term is None else down_add_body, out_shape=ja...  17.9 us
    all_to_all x1, blocking collectives, local(): lax.all_to_all(blocks, 'grp', split_axis=0, concat_axis=0, tiled=True)  16.9 us
    all_to_all x2, starting transfers between devices, local(): lax.all_to_all(sent[m], 'ep', split_axis=0, concat_axis=0, tiled=True)  14.8 us
    pallas_call x2, Pallas kernels, hidden_of(): pl.pallas_call(hidden_body, out_shape=jax.ShapeDtypeStruct((slots, width)...  13.7 us
    all_to_all x2, starting transfers between devices, local(): back = lax.all_to_all(out, 'ep', split_axis=0, concat_axis=0, tiled=True)  12.3 us
    dot_general x4, matrix products, dot(): return jnp.dot(a, b, preferred_element_type=F32)  7.06 us
  transfers between devices with their start and end apart: 8, of which 5 were waited for; matrix products, arithmetic and copies ran while one was open for 2% of the time, Pallas kernels for 19%

profile of v1, /device:TPU:2, one launch (start us, length us, event | category | flops | bytes accessed | tf_op | source)
XLA Modules:
  0.0 164.3 jit_solution(7253784583251648857)
XLA Ops:
  0.0 0.8 fusion.28
  0.8 0.1 copy.27
  0.9 0.1 eq.56
  1.0 0.1 fusion.11
  1.1 0.2 reduce_window_sum.17
  1.3 0.2 select_reduce_fusion.3
  1.4 0.1 reduce_sum.71
  1.5 0.8 fusion.29
  2.4 0.1 copy.22
  2.5 0.1 select_reduce_fusion.1
  2.6 2.8 %fusion = bf16[32,8,3584]{2,1,0:T(8,128)(2,1)} fusion(bf16[32,3584]{1,0:T(8,128)(2,1)} %param.6, bf16[256,16]{0,1:T(8,128)(2,1)S(1)} %get-tuple-element.6), kind=kOutput, calls=%fused_computation.2 | convolution fusion | flops 30277632 | bytes 1957888 | tf_op jit(solution)/shard_map/dot_general | solution.py:17
  5.4 9.1 %all-to-all-start = ((bf16[32,8,3584]{2,1,0:T(8,128)(2,1)}), bf16[32,8,3584]{2,1,0:T(8,128)(2,1)S(1)}, u32[]{:S(2)}, u32[]{:S(2)}) async-start(bf16[32,8,3584]{2,1,0:T(8,128)(2,1)} %fusion), calls=%async_computation | async-start | bytes 3670016 | tf_op jit(solution)/shard_map/all_to_all | solution.py:141
  14.5 0.1 copy.28
  14.6 0.1 eq.63
  14.7 0.1 fusion.10
  14.8 0.2 reduce_window_sum.18
  15.0 0.2 select_reduce_fusion.2
  15.1 0.1 reduce_sum.75
  15.2 0.1 copy.24
  15.3 0.2 select_reduce_fusion
  15.5 24.4 %all-to-all-done = bf16[32,8,3584]{2,1,0:T(8,128)(2,1)S(1)} async-done(((bf16[32,8,3584]{2,1,0:T(8,128)(2,1)}), bf16[32,8,3584]{2,1,0:T(8,128)(2,1)S(1)}, u32[]{:S(2)}, u32[]{:S(2)}) %all-to-all-start) | async-done | bytes 1835040 | tf_op jit(solution)/shard_map/all_to_all | solution.py:141
  39.9 0.0 collective-permute-start
  39.9 0.0 copy-done.2
  39.9 1.9 %fusion.1 = bf16[32,8,3584]{2,1,0:T(8,128)(2,1)} fusion(bf16[32,3584]{1,0:T(8,128)(2,1)S(1)} %copy-done.2, bf16[256,16]{0,1:T(8,128)(2,1)S(1)} %get-tuple-element.8), kind=kOutput, calls=%fused_computation.3 | convolution fusion | flops 30277632 | bytes 1957888 | tf_op jit(solution)/shard_map/dot_general | solution.py:17
  41.8 5.7 %all-to-all-start.2 = ((bf16[32,8,3584]{2,1,0:T(8,128)(2,1)}), bf16[32,8,3584]{2,1,0:T(8,128)(2,1)}, u32[]{:S(2)}, u32[]{:S(2)}) async-start(bf16[32,8,3584]{2,1,0:T(8,128)(2,1)} %fusion.1), calls=%async_computation.2 | async-start | bytes 3670016 | tf_op jit(solution)/shard_map/all_to_all | solution.py:141
  47.5 0.0 collective-permute-done.peer
  47.6 6.8 %hidden.2 = bf16[256,256]{1,0:T(8,128)(2,1)} custom-call(s32[1]{0:T(128)} %bitcast.1.t, bf16[256,3584]{1,0:T(8,128)(2,1)} %bitcast.51, bf16[256,3584]{1,0:T(8,128)(2,1)} %collective-permute-done.peer, bf16[7168,256]{1,0:T(8,128)(2,1)} %bitcast.46, bf16[7168,256]{1,0:T(8,128)(2,1)} %bitcast.48), custom_call_target="tpu_custom_call" | custom-call | tf_op jit(solution)/shard_map/hidden/pallas_call | solution.py:65
  54.4 4.3 %down.2 = bf16[256,3584]{1,0:T(8,128)(2,1)} custom-call(s32[1]{0:T(128)S(6)} %sub.27.t, bf16[256,256]{1,0:T(8,128)(2,1)} %hidden.2, bf16[256,7168]{1,0:T(8,128)(2,1)} %bitcast.42), custom_call_target="tpu_custom_call" | custom-call | tf_op jit(solution)/shard_map/down/pallas_call | solution.py:101
  58.7 0.2 collective-permute-start.1
  58.9 16.2 %all-to-all-done.2 = bf16[32,8,3584]{2,1,0:T(8,128)(2,1)} async-done(((bf16[32,8,3584]{2,1,0:T(8,128)(2,1)}), bf16[32,8,3584]{2,1,0:T(8,128)(2,1)}, u32[]{:S(2)}, u32[]{:S(2)}) %all-to-all-start.2) | async-done | bytes 1835040 | tf_op jit(solution)/shard_map/all_to_all | solution.py:141
  75.1 0.0 collective-permute-start.2
  75.1 0.0 collective-permute-done.1.term
  75.1 1.3 copy-done.1
  76.4 4.7 %down_add.2 = bf16[256,3584]{1,0:T(8,128)(2,1)} custom-call(s32[1]{0:T(128)} %bitcast.1.t, bf16[256,256]{1,0:T(8,128)(2,1)} %hidden.2, bf16[256,7168]{1,0:T(8,128)(2,1)} %bitcast.43, bf16[256,3584]{1,0:T(8,128)(2,1)} %copy-done.1), custom_call_target="tpu_custom_call" | custom-call | tf_op jit(solution)/shard_map/down_add/pallas_call | solution.py:101
  81.0 6.3 %all-to-all-start.1 = ((bf16[32,8,3584]{2,1,0:T(8,128)(2,1)}), bf16[32,8,3584]{2,1,0:T(8,128)(2,1)S(1)}, u32[]{:S(2)}, u32[]{:S(2)}) async-start(bf16[32,8,3584]{2,1,0:T(8,128)(2,1)} %bitcast.53), calls=%async_computation.1 | async-start | bytes 3670016 | tf_op jit(solution)/shard_map/all_to_all | solution.py:146
  87.3 0.0 collective-permute-done.2.peer
  87.3 6.9 %hidden.3 = bf16[256,256]{1,0:T(8,128)(2,1)} custom-call(s32[1]{0:T(128)} %bitcast.1.t, bf16[256,3584]{1,0:T(8,128)(2,1)} %bitcast.11.own, bf16[256,3584]{1,0:T(8,128)(2,1)} %collective-permute-done.2.peer, bf16[7168,256]{1,0:T(8,128)(2,1)} %bitcast.47, bf16[7168,256]{1,0:T(8,128)(2,1)} %bitcast.49), custom_call_target="tpu_custom_call" | custom-call | tf_op jit(solution)/shard_map/hidden/pallas_call | solution.py:65
  94.2 4.3 %down.3 = bf16[256,3584]{1,0:T(8,128)(2,1)} custom-call(s32[1]{0:T(128)S(6)} %sub.27.t, bf16[256,256]{1,0:T(8,128)(2,1)} %hidden.3, bf16[256,7168]{1,0:T(8,128)(2,1)} %bitcast.44), custom_call_target="tpu_custom_call" | custom-call | tf_op jit(solution)/shard_map/down/pallas_call | solution.py:101
  98.5 0.0 collective-permute-start.3
  98.5 4.1 %collective-permute-done.3.term = bf16[256,3584]{1,0:T(8,128)(2,1)} collective-permute-done((bf16[256,3584]{1,0:T(8,128)(2,1)}, bf16[256,3584]{1,0:T(8,128)(2,1)}, u32[]{:S(2)}, u32[]{:S(2)}) %collective-permute-start.3) | collective-permute-done | bytes 1835040 | tf_op jit(solution)/shard_map/ppermute | solution.py:21
  102.6 4.6 %down_add.3 = bf16[256,3584]{1,0:T(8,128)(2,1)} custom-call(s32[1]{0:T(128)} %bitcast.1.t, bf16[256,256]{1,0:T(8,128)(2,1)} %hidden.3, bf16[256,7168]{1,0:T(8,128)(2,1)} %bitcast.45, bf16[256,3584]{1,0:T(8,128)(2,1)} %collective-permute-done.3.term), custom_call_target="tpu_custom_call" | custom-call | tf_op jit(solution)/shard_map/down_add/pallas_call | solution.py:101
  107.2 6.9 %all-to-all-done.1 = bf16[32,8,3584]{2,1,0:T(8,128)(2,1)S(1)} async-done(((bf16[32,8,3584]{2,1,0:T(8,128)(2,1)}), bf16[32,8,3584]{2,1,0:T(8,128)(2,1)S(1)}, u32[]{:S(2)}, u32[]{:S(2)}) %all-to-all-start.1) | async-done | bytes 1835040 | tf_op jit(solution)/shard_map/all_to_all | solution.py:146
  114.2 6.0 %all-to-all-start.3 = ((bf16[32,8,3584]{2,1,0:T(8,128)(2,1)}), bf16[32,8,3584]{2,1,0:T(8,128)(2,1)}, u32[]{:S(2)}, u32[]{:S(2)}) async-start(bf16[32,8,3584]{2,1,0:T(8,128)(2,1)} %bitcast.52), calls=%async_computation.3 | async-start | bytes 3670016 | tf_op jit(solution)/shard_map/all_to_all | solution.py:146
  120.2 0.4 fusion.4
  120.7 24.1 %all-to-all-done.3 = bf16[32,8,3584]{2,1,0:T(8,128)(2,1)} async-done(((bf16[32,8,3584]{2,1,0:T(8,128)(2,1)}), bf16[32,8,3584]{2,1,0:T(8,128)(2,1)}, u32[]{:S(2)}, u32[]{:S(2)}) %all-to-all-start.3) | async-done | bytes 1835040 | tf_op jit(solution)/shard_map/all_to_all | solution.py:146
  144.8 1.9 %fusion.2 = f32[48,3584]{1,0:T(8,128)S(1)} fusion(bf16[32,8,3584]{2,1,0:T(8,128)(2,1)} %all-to-all-done.3, bf16[16,256]{1,0:T(8,128)(2,1)S(1)} %get-tuple-element.13, bf16[16,256]{1,0:T(8,128)(2,1)S(1)} %get-tuple-element.14, bf16[16,256]{1,0:T(8,128)(2,1)S(1)} %get-tuple-element.12), kind=kOutput, calls=%fused_computation.4 | convolution fusion | flops 88154112 | bytes 2547712 | tf_op jit(solution)/shard_map/dot_general | solution.py:17
  146.8 16.9 %all_to_all.25 = bf16[4,32,896]{2,1,0:T(8,128)(2,1)S(1)} all-to-all(bf16[4,32,896]{2,1,0:T(8,128)(2,1)S(1)} %maximum_bitcast_fusion), channel_id=1, replica_groups=mesh['grp'=4,'ep'=32,'tp'=2] {'grp'}, dimensions={0} | all-to-all | bytes 458752 | tf_op jit(solution)/shard_map/all_to_all | solution.py:151
  163.7 0.7 reduce_sum.78
  (12 shorter events, 0.2 us)
Async XLA Ops:
  5.4 34.5 %copy-start.2 = (bf16[32,3584]{1,0:T(8,128)(2,1)S(1)}, bf16[32,3584]{1,0:T(8,128)(2,1)}, u32[]{:S(2)}) copy-start(bf16[32,3584]{1,0:T(8,128)(2,1)} %param.6) | copy-start | bytes 688132
  5.4 34.5 %all-to-all-start = ((bf16[32,8,3584]{2,1,0:T(8,128)(2,1)}), bf16[32,8,3584]{2,1,0:T(8,128)(2,1)S(1)}, u32[]{:S(2)}, u32[]{:S(2)}) async-start(bf16[32,8,3584]{2,1,0:T(8,128)(2,1)} %fusion), calls=%async_computation | async-start | bytes 3670016 | tf_op jit(solution)/shard_map/all_to_all | solution.py:141
  39.9 1.9 %copy-start = (bf16[32,8,3584]{2,1,0:T(8,128)(2,1)}, bf16[32,8,3584]{2,1,0:T(8,128)(2,1)S(1)}, u32[]{:S(2)}) copy-start(bf16[32,8,3584]{2,1,0:T(8,128)(2,1)S(1)} %all-to-all-done) | copy-start | bytes 5505028
  39.9 7.7 %collective-permute-start = (bf16[256,3584]{1,0:T(8,128)(2,1)S(1)}, bf16[256,3584]{1,0:T(8,128)(2,1)}, u32[]{:S(2)}, u32[]{:S(2)}) collective-permute-start(bf16[256,3584]{1,0:T(8,128)(2,1)S(1)} %bitcast.50), channel_id=1, source_target_pairs={{0,1},{1,0},{2,3},{3,2},{4,5},{5,4},{6,7},{7,6},{8,9},{9,8},{10,11... | collective-permute-start | bytes 5505032 | tf_op jit(solution)/shard_map/ppermute | solution.py:21
  41.8 33.3 %all-to-all-start.2 = ((bf16[32,8,3584]{2,1,0:T(8,128)(2,1)}), bf16[32,8,3584]{2,1,0:T(8,128)(2,1)}, u32[]{:S(2)}, u32[]{:S(2)}) async-start(bf16[32,8,3584]{2,1,0:T(8,128)(2,1)} %fusion.1), calls=%async_computation.2 | async-start | bytes 3670016 | tf_op jit(solution)/shard_map/all_to_all | solution.py:141
  58.7 16.4 %collective-permute-start.1 = (bf16[256,3584]{1,0:T(8,128)(2,1)}, bf16[256,3584]{1,0:T(8,128)(2,1)S(1)}, u32[]{:S(2)}, u32[]{:S(2)}) collective-permute-start(bf16[256,3584]{1,0:T(8,128)(2,1)} %down.2), channel_id=1, source_target_pairs={{0,1},{1,0},{2,3},{3,2},{4,5},{5,4},{6,7},{7,6},{8,9},{9,8},{10,11... | collective-permute-start | bytes 5505032 | tf_op jit(solution)/shard_map/ppermute | solution.py:21
  75.1 12.3 %collective-permute-start.2 = (bf16[256,3584]{1,0:T(8,128)(2,1)}, bf16[256,3584]{1,0:T(8,128)(2,1)}, u32[]{:S(2)}, u32[]{:S(2)}) collective-permute-start(bf16[256,3584]{1,0:T(8,128)(2,1)} %bitcast.11.own), channel_id=1, source_target_pairs={{0,1},{1,0},{2,3},{3,2},{4,5},{5,4},{6,7},{7,6},{8,9},{9,8},{10,11... | collective-permute-start | bytes 5505032 | tf_op jit(solution)/shard_map/ppermute | solution.py:21
  75.1 1.3 copy-start.1
  81.0 33.1 %all-to-all-start.1 = ((bf16[32,8,3584]{2,1,0:T(8,128)(2,1)}), bf16[32,8,3584]{2,1,0:T(8,128)(2,1)S(1)}, u32[]{:S(2)}, u32[]{:S(2)}) async-start(bf16[32,8,3584]{2,1,0:T(8,128)(2,1)} %bitcast.53), calls=%async_computation.1 | async-start | bytes 3670016 | tf_op jit(solution)/shard_map/all_to_all | solution.py:146
  98.5 4.1 %collective-permute-start.3 = (bf16[256,3584]{1,0:T(8,128)(2,1)}, bf16[256,3584]{1,0:T(8,128)(2,1)}, u32[]{:S(2)}, u32[]{:S(2)}) collective-permute-start(bf16[256,3584]{1,0:T(8,128)(2,1)} %down.3), channel_id=1, source_target_pairs={{0,1},{1,0},{2,3},{3,2},{4,5},{5,4},{6,7},{7,6},{8,9},{9,8},{10,11... | collective-permute-start | bytes 5505032 | tf_op jit(solution)/shard_map/ppermute | solution.py:21
  114.2 30.6 %all-to-all-start.3 = ((bf16[32,8,3584]{2,1,0:T(8,128)(2,1)}), bf16[32,8,3584]{2,1,0:T(8,128)(2,1)}, u32[]{:S(2)}, u32[]{:S(2)}) async-start(bf16[32,8,3584]{2,1,0:T(8,128)(2,1)} %bitcast.52), calls=%async_computation.3 | async-start | bytes 3670016 | tf_op jit(solution)/shard_map/all_to_all | solution.py:146

commit v2 on v0

v2 whole, which is shorter than its diff:
```python
import jax
import jax.numpy as jnp
from jax import lax
from jax.experimental import pallas as pl
from jax.experimental.pallas import tpu as pltpu
from jax.sharding import PartitionSpec as P

EXPERTS = 32
CAP = 8
TOK_MB = 16
INTERPRET = False
BF = jnp.bfloat16
F32 = jnp.float32


def dot(a, b):
    return jnp.dot(a, b, preferred_element_type=F32)


def other_core(a):
    return lax.ppermute(a, "tp", [(0, 1), (1, 0)])


def iota(shape, dim):
    return lax.broadcasted_iota(jnp.int32, shape, dim)


def bits(mask):
    return mask.astype(F32).astype(BF)


def place_body(ids_t, tokens, out, placing):
    @pl.when(pl.program_id(0) == 0)
    def _():
        top, count = ids_t.shape
        rows = placing.shape[0]
        per = rows // EXPERTS
        expert = iota((EXPERTS, count), 0)
        chosen = jnp.zeros((EXPERTS, count), F32)
        for k in range(top):
            chosen += (ids_t[k : k + 1, :] == expert).astype(F32)
        i, j = iota((count, count), 0), iota((count, count), 1)
        before = dot(chosen.astype(BF), bits((i // TOK_MB == j // TOK_MB) & (i < j)))
        target = jnp.where(chosen > 0.5, before, -1.0).astype(BF)
        of_row = bits(iota((rows, EXPERTS), 0) // per == iota((rows, EXPERTS), 1))
        target = dot(of_row, target)
        r, c = iota((rows, count), 0), iota((rows, count), 1)
        hit = (target == (r % CAP).astype(F32)) & (c // TOK_MB == r % per // CAP)
        placing[...] = bits(hit)

    out[...] = dot(placing[...], tokens[...]).astype(BF)


def place(tokens, expert_ids):
    count, width = tokens.shape
    rows = EXPERTS * (count // TOK_MB) * CAP
    block = width // 4
    return pl.pallas_call(
        place_body,
        out_shape=jax.ShapeDtypeStruct((rows, width), BF),
        grid=(4,),
        in_specs=[
            pl.BlockSpec(expert_ids.shape[::-1], lambda i: (0, 0)),
            pl.BlockSpec((count, block), lambda i: (0, i)),
        ],
        out_specs=pl.BlockSpec((rows, block), lambda i: (0, i)),
        scratch_shapes=[pltpu.VMEM((rows, count), BF)],
        interpret=INTERPRET,
        name="place",
    )(jnp.transpose(expert_ids), tokens)


def mixing(gates, expert_ids):
    count = gates.shape[0]
    blocks = count // TOK_MB
    onehot = (expert_ids[:, :, None] == lax.iota(jnp.int32, EXPERTS)).astype(F32)
    chosen = jnp.sum(onehot, axis=1)
    weight = jnp.sum(onehot * gates[:, :, None], axis=1)
    earlier = (iota((TOK_MB, TOK_MB), 1) < iota((TOK_MB, TOK_MB), 0)).astype(F32)
    before = jnp.einsum("ts,bse->bte", earlier, chosen.reshape(blocks, TOK_MB, EXPERTS))
    target = jnp.where(chosen > 0.5, before.reshape(count, EXPERTS), -1.0)[:, :, None]
    column = iota((1, 1, blocks * CAP), 2)
    own = column // CAP == iota((count, 1, 1), 0) // TOK_MB
    hit = own & (target == (column % CAP).astype(F32))
    mix = jnp.where(hit, weight[:, :, None], 0.0).reshape(count, -1)
    high = lax.reduce_precision(mix, 8, 7)
    middle = lax.reduce_precision(mix - high, 8, 7)
    return jnp.concatenate([high, middle, mix - high - middle], axis=0).astype(BF)


def mix_body(mix, rows, out):
    total = dot(mix[...], rows[...])
    n = total.shape[0] // 3
    out[...] = (total[:n] + total[n : 2 * n] + total[2 * n :]).astype(BF)[None]


def mix_rows(mix, rows):
    slots, width = rows.shape
    count = mix.shape[0] // 3
    block = width // 4
    return pl.pallas_call(
        mix_body,
        out_shape=jax.ShapeDtypeStruct((4, count, block), BF),
        grid=(4,),
        in_specs=[
            pl.BlockSpec(mix.shape, lambda i: (0, 0)),
            pl.BlockSpec((slots, block), lambda i: (0, i)),
        ],
        out_specs=pl.BlockSpec((1, count, block), lambda i: (i, 0, 0)),
        interpret=INTERPRET,
        name="mix",
    )(mix, rows)


def down_body(t, hidden, weight, out):
    out[...] = dot(hidden[...], weight[...]).astype(BF)


def down_add_body(t, hidden, weight, low, high, out):
    term = jnp.where(pl.program_id(0) < 2, low[...], high[...])
    out[...] = (dot(hidden[...], weight[...]) + term.astype(F32)).astype(BF)


def down(hidden, weight, which, first):
    slots, inner = hidden.shape
    block = weight.shape[1] // 8
    return pl.pallas_call(
        down_body,
        out_shape=jax.ShapeDtypeStruct((slots, 2 * block), BF),
        grid_spec=pltpu.PrefetchScalarGridSpec(
            num_scalar_prefetch=1,
            grid=(2,),
            in_specs=[
                pl.BlockSpec((slots, inner), lambda i, t: (0, 0)),
                pl.BlockSpec((inner, block), lambda i, t: (0, 2 * (first + i) + t[0])),
            ],
            out_specs=pl.BlockSpec((slots, block), lambda i, t: (0, i)),
        ),
        compiler_params=pltpu.CompilerParams(vmem_limit_bytes=12 << 20),
        interpret=INTERPRET,
        name="down",
    )(which, hidden, weight)


def down_add(hidden, weight, which, low, high):
    slots, inner = hidden.shape
    block = weight.shape[1] // 8
    return pl.pallas_call(
        down_add_body,
        out_shape=jax.ShapeDtypeStruct((slots, 4 * block), BF),
        grid_spec=pltpu.PrefetchScalarGridSpec(
            num_scalar_prefetch=1,
            grid=(4,),
            in_specs=[
                pl.BlockSpec((slots, inner), lambda i, t: (0, 0)),
                pl.BlockSpec((inner, block), lambda i, t: (0, 2 * i + t[0])),
                pl.BlockSpec((slots, block), lambda i, t: (0, jnp.minimum(i, 1))),
                pl.BlockSpec((slots, block), lambda i, t: (0, jnp.maximum(i - 2, 0))),
            ],
            out_specs=pl.BlockSpec((slots, block), lambda i, t: (0, i)),
        ),
        compiler_params=pltpu.CompilerParams(vmem_limit_bytes=16 << 20),
        interpret=INTERPRET,
        name="down_add",
    )(which, hidden, weight, low, high)


def local(tokens, gates, expert_ids, gate_weight, up_weight, down_weight):
    downw = down_weight[0]
    t = lax.axis_index("tp").astype(jnp.int32)
    width = tokens.shape[1]
    gate = gate_weight.reshape(2, width, -1)
    up = up_weight.reshape(2, width, -1)

    def half(weight, which):
        return lax.dynamic_index_in_dim(weight, which, 0, keepdims=False)

    sent = place(tokens, expert_ids)
    mix = mixing(gates, expert_ids)
    slots = sent.shape[0]
    sent = sent.reshape(EXPERTS, -1, width)
    rows = lax.all_to_all(sent, "ep", split_axis=0, concat_axis=0, tiled=True)
    rows = rows.reshape(slots, width)
    peer = other_core(rows)
    g, u = dot(rows, half(gate, t)), dot(rows, half(up, t))
    g, u = g + dot(peer, half(gate, 1 - t)), u + dot(peer, half(up, 1 - t))
    hidden = (g * jax.nn.sigmoid(g) * u).astype(BF)
    which = t.reshape(1)
    low = other_core(down(hidden, downw, 1 - which, 0))
    high = other_core(down(hidden, downw, 1 - which, 2))
    out = down_add(hidden, downw, which, low, high).reshape(EXPERTS, -1, width)
    back = lax.all_to_all(out, "ep", split_axis=0, concat_axis=0, tiled=True)
    blocks = mix_rows(mix, back.reshape(slots, width))
    shares = lax.all_to_all(blocks, "grp", split_axis=0, concat_axis=0, tiled=True)
    return jnp.sum(shares.astype(F32), axis=0).astype(BF)


def solution(mesh):
    placed = (
        P("ep", "tp"),
        P("ep", None),
        P("ep", None),
        P("ep", None, ("grp", "tp")),
        P("ep", None, ("grp", "tp")),
        P("ep", ("grp", "tp"), None),
    )
    return jax.shard_map(
        local, mesh=mesh, in_specs=placed, out_specs=P("ep", ("grp", "tp")), check_vma=False
    )
```

time: 239 us -> 171 us (0.72)
  waiting for transfers between devices: 115 us -> 58.5 us
  blocking collectives: 28.8 us -> 71.1 us
  matrix products: 32.9 us -> 13.7 us
  starting transfers between devices: 25.6 us -> 6.7 us
  local copies, waits for them, and re-layouts: 19.7 us -> 2.62 us
  Pallas kernels: 0 us -> 13.9 us
  between operations: 13.3 us -> 0.2 us
    unnamed x6 -> x0, waiting for transfers between devices: 79.9 us -> none
    all_to_all x1 -> x2, blocking collectives: 28.8 us -> 71.1 us  [the longest x1 53.9 us: local(): rows = lax.all_to_all(sent, 'ep', split_axis=0, concat_axis=0, tiled=True)]
    all_to_all x3 -> x1, starting transfers between devices: 25.3 us -> 6 us  [local(): back = lax.all_to_all(out, 'ep', split_axis=0, concat_axis=0, tiled=True)]
    dot_general x8 -> x5, matrix products: 32.9 us -> 13.7 us  [the longest x4 13.6 us: dot(): return jnp.dot(a, b, preferred_element_type=F32)]
    all_to_all x3 -> x1, waiting for transfers between devices: 35.1 us -> 52.6 us  [local(): back = lax.all_to_all(out, 'ep', split_axis=0, concat_axis=0, tiled=True)]
    unnamed x10 -> x14, local copies, waits for them, and re-layouts: 17.6 us -> 2 us
    pallas_call x0 -> x5, Pallas kernels: none -> 13.9 us  [the longest x1 4.6 us: place(): pl.pallas_call(place_body, out_shape=jax.ShapeDtypeStruct((rows, width),...]
    ppermute x0 -> x3, waiting for transfers between devices: none -> 5.94 us  [other_core(): return lax.ppermute(a, 'tp', [(0, 1), (1, 0)])]
  transfers between devices with their start and end apart: 7 -> 4, of which waited for: 4 -> 3; matrix products, arithmetic and copies ran while one was open for 20% -> 5% of each run, Pallas kernels for 0% -> 0%
where the time goes in v2:
time: 171 us; the launch traced here: 168 us
  blocking collectives  71.1 us (42%)
  waiting for transfers between devices  58.5 us (34%)
  Pallas kernels  13.9 us (8%)
  matrix products  13.7 us (8%)
  starting transfers between devices  6.7 us (4%)
  local copies, waits for them, and re-layouts  2.62 us (2%)
    all_to_all x1, blocking collectives, local(): rows = lax.all_to_all(sent, 'ep', split_axis=0, concat_axis=0, tiled=True)  53.9 us
    all_to_all x1, waiting for transfers between devices, local(): back = lax.all_to_all(out, 'ep', split_axis=0, concat_axis=0, tiled=True)  52.6 us
    all_to_all x1, blocking collectives, local(): lax.all_to_all(blocks, 'grp', split_axis=0, concat_axis=0, tiled=True)  17.3 us
    dot_general x4, matrix products, dot(): return jnp.dot(a, b, preferred_element_type=F32)  13.6 us
    all_to_all x1, starting transfers between devices, local(): back = lax.all_to_all(out, 'ep', split_axis=0, concat_axis=0, tiled=True)  6 us
    ppermute x3, waiting for transfers between devices, other_core(): return lax.ppermute(a, 'tp', [(0, 1), (1, 0)])  5.94 us
    pallas_call x1, Pallas kernels, place(): pl.pallas_call(place_body, out_shape=jax.ShapeDtypeStruct((rows, width),...  4.6 us
    pallas_call x1, Pallas kernels, mix_rows(): pl.pallas_call(mix_body, out_shape=jax.ShapeDtypeStruct((4, count, block)...  4.28 us
  transfers between devices with their start and end apart: 4, of which 3 were waited for; matrix products, arithmetic and copies ran while one was open for 5% of the time, Pallas kernels for 0%

profile of v2, /device:TPU:2, one launch (start us, length us, event | category | flops | bytes accessed | tf_op | source)
XLA Modules:
  0.0 168.4 jit_solution(12359723909047039575)
XLA Ops:
  0.0 4.6 %place.1 = bf16[512,3584]{1,0:T(8,128)(2,1)} custom-call(s32[8,32]{1,0:T(8,128)} %bitcast.52, bf16[32,3584]{1,0:T(8,128)(2,1)} %tokens.1), custom_call_target="tpu_custom_call" | custom-call | tf_op jit(solution)/shard_map/place/pallas_call | solution.py:58
  4.6 53.9 %all_to_all.15 = bf16[32,16,3584]{2,1,0:T(8,128)(2,1)} all-to-all(bf16[32,16,3584]{2,1,0:T(8,128)(2,1)} %bitcast.47), channel_id=1, replica_groups=mesh['grp'=4,'ep'=32,'tp'=2] {'ep'}, dimensions={0} | all-to-all | bytes 7340032 | tf_op jit(solution)/shard_map/all_to_all | solution.py:182
  58.5 0.0 collective-permute-start
  58.5 0.0 copy-start.5
  58.5 3.9 %fusion.6 = f32[512,256]{1,0:T(8,128)S(1)} fusion(bf16[512,3584]{1,0:T(8,128)(2,1)} %bitcast.10, bf16[2,3584,256]{2,1,0:T(8,128)(2,1)} %bitcast.53, s32[]{:T(128)S(6)} %select_n.59), kind=kOutput, calls=%fused_computation.6 | convolution fusion | flops 939524096 | bytes 6029316 | tf_op jit(solution)/shard_map/dot_general | solution.py:17
  62.3 0.0 copy-start.4
  62.3 0.0 copy-done.5
  62.4 3.3 %fusion.2 = f32[512,256]{1,0:T(8,128)S(1)} fusion(bf16[512,3584]{1,0:T(8,128)(2,1)} %bitcast.10, bf16[2,3584,256]{2,1,0:T(8,128)(2,1)S(1)} %bitcast.55, s32[]{:T(128)S(6)} %select_n.59), kind=kOutput, calls=%fused_computation.2 | convolution fusion | flops 939524096 | bytes 6029316 | tf_op jit(solution)/shard_map/dot_general | solution.py:17
  65.7 0.0 collective-permute-done
  65.7 0.0 copy-done.4
  65.7 3.2 %fusion.12 = f32[512,256]{1,0:T(8,128)S(1)} fusion(f32[512,256]{1,0:T(8,128)S(1)} %fusion.6, bf16[512,3584]{1,0:T(8,128)(2,1)} %collective-permute-done, bf16[2,3584,256]{2,1,0:T(8,128)(2,1)S(1)} %bitcast.54, s32[]{:T(128)S(6)} %select_n.60), kind=kOutput, calls=%fused_computation.12 | convolution fusion | flops 939655168 | bytes 6553604 | tf_op jit(solution)/shard_map/dot_general | solution.py:17
  68.8 0.0 copy-start
  68.9 3.3 %multiply_convert_fusion.hidden = bf16[512,256]{1,0:T(8,128)(2,1)S(1)} fusion(f32[512,256]{1,0:T(8,128)S(1)} %fusion.12, f32[512,256]{1,0:T(8,128)S(1)} %fusion.2, bf16[512,3584]{1,0:T(8,128)(2,1)} %collective-permute-done, bf16[2,3584,256]{2,1,0:T(8,128)(2,1)S(1)} %bitcast.56, s32[]{:T(128)S(6)} %select_n.60), kind=kOutput, calls=%fused_computation.14 | convolution fusion | flops 940441600 | bytes 6815748 | tf_op jit(solution)/shard_map/dot_general | solution.py:17
  72.2 0.0 copy-done
  72.2 1.2 down.3
  73.4 1.2 down.2
  74.5 0.6 collective-permute-start.2
  75.1 0.1 collective-permute-start.1
  75.2 3.3 %collective-permute-done.2.high = bf16[512,1792]{1,0:T(8,128)(2,1)S(1)} collective-permute-done((bf16[512,1792]{1,0:T(8,128)(2,1)S(1)}, bf16[512,1792]{1,0:T(8,128)(2,1)S(1)}, u32[]{:S(2)}, u32[]{:S(2)}) %collective-permute-start.2) | collective-permute-done | bytes 1835040 | tf_op jit(solution)/shard_map/ppermute | solution.py:21
  78.5 2.6 %collective-permute-done.1.low = bf16[512,1792]{1,0:T(8,128)(2,1)S(1)} collective-permute-done((bf16[512,1792]{1,0:T(8,128)(2,1)S(1)}, bf16[512,1792]{1,0:T(8,128)(2,1)S(1)}, u32[]{:S(2)}, u32[]{:S(2)}) %collective-permute-start.1) | collective-permute-done | bytes 1835040 | tf_op jit(solution)/shard_map/ppermute | solution.py:21
  81.2 2.7 %down_add.1 = bf16[512,3584]{1,0:T(8,128)(2,1)S(1)} custom-call(s32[1]{0:T(128)} %bitcast.7.t, bf16[512,256]{1,0:T(8,128)(2,1)S(1)} %multiply_convert_fusion.hidden, bf16[256,7168]{1,0:T(8,128)(2,1)S(1)} %bitcast.45, bf16[512,1792]{1,0:T(8,128)(2,1)S(1)} %collective-permute-done.1.low, bf16[512,1792]{1,0:T(8,128)(2,1)S(1)} %collective-permute-done.2.high), custom_call_target="tpu_custom_call" | custom-call | tf_op jit(solution)/shard_map/down_add/pallas_call | solution.py:148
  83.8 0.0 copy-start.1
  83.8 1.8 %copy-done.1 = bf16[512,3584]{1,0:T(8,128)(2,1)} copy-done((bf16[512,3584]{1,0:T(8,128)(2,1)}, bf16[512,3584]{1,0:T(8,128)(2,1)S(1)}, u32[]{:S(2)}) %copy-start.1) | copy-done | bytes 3670040
  85.7 0.0 copy-start.2
  85.7 0.0 copy-start.3
  85.7 6.0 %all-to-all-start.1 = ((bf16[32,16,3584]{2,1,0:T(8,128)(2,1)}), bf16[32,16,3584]{2,1,0:T(8,128)(2,1)}, u32[]{:S(2)}, u32[]{:S(2)}) async-start(bf16[32,16,3584]{2,1,0:T(8,128)(2,1)} %bitcast.46), calls=%async_computation.1 | async-start | bytes 7340032 | tf_op jit(solution)/shard_map/all_to_all | solution.py:192
  91.7 0.0 copy-done.2
  91.7 0.1 copy.15
  91.8 0.0 copy-done.3
  91.8 0.1 copy.19
  91.9 0.2 convert_reduce_fusion
  92.0 0.1 fusion.20
  92.1 0.1 copy.16
  92.2 0.1 copy.17
  92.3 0.1 copy.20
  92.4 0.1 copy.21
  92.6 0.1 broadcast_compare_fusion
  92.7 0.1 copy.18
  92.8 0.1 eq.62
  92.9 0.6 pad_maximum_fusion.mix
  93.6 52.6 %all-to-all-done.1 = bf16[32,16,3584]{2,1,0:T(8,128)(2,1)} async-done(((bf16[32,16,3584]{2,1,0:T(8,128)(2,1)}), bf16[32,16,3584]{2,1,0:T(8,128)(2,1)}, u32[]{:S(2)}, u32[]{:S(2)}) %all-to-all-start.1) | async-done | bytes 3670048 | tf_op jit(solution)/shard_map/all_to_all | solution.py:192
  146.2 4.3 %mix.1 = bf16[4,32,896]{2,1,0:T(8,128)(2,1)} custom-call(bf16[96,512]{1,0:T(8,128)(2,1)} %pad_maximum_fusion.mix, bf16[512,3584]{1,0:T(8,128)(2,1)} %bitcast.19.rows), custom_call_target="tpu_custom_call" | custom-call | tf_op jit(solution)/shard_map/mix/pallas_call | solution.py:101
  150.5 17.3 %all_to_all.16 = bf16[4,32,896]{2,1,0:T(8,128)(2,1)S(1)} all-to-all(bf16[4,32,896]{2,1,0:T(8,128)(2,1)} %mix.1), channel_id=1, replica_groups=mesh['grp'=4,'ep'=32,'tp'=2] {'grp'}, dimensions={0} | all-to-all | bytes 458752 | tf_op jit(solution)/shard_map/all_to_all | solution.py:194
  167.8 0.7 reduce_sum.32
  (9 shorter events, 0.1 us)
Async XLA Ops:
  58.5 7.2 %collective-permute-start = (bf16[512,3584]{1,0:T(8,128)(2,1)}, bf16[512,3584]{1,0:T(8,128)(2,1)}, u32[]{:S(2)}, u32[]{:S(2)}) collective-permute-start(bf16[512,3584]{1,0:T(8,128)(2,1)} %bitcast.10), channel_id=1, source_target_pairs={{0,1},{1,0},{2,3},{3,2},{4,5},{5,4},{6,7},{7,6},{8,9},{9,8},{10,11... | collective-permute-start | bytes 11010056 | tf_op jit(solution)/shard_map/ppermute | solution.py:21
  58.5 3.9 %copy-start.5 = (bf16[1,7168,256]{2,1,0:T(8,128)(2,1)S(1)}, bf16[1,7168,256]{2,1,0:T(8,128)(2,1)}, u32[]{:S(2)}) copy-start(bf16[1,7168,256]{2,1,0:T(8,128)(2,1)} %param.10) | copy-start | bytes 11010052
  62.3 3.3 %copy-start.4 = (bf16[1,7168,256]{2,1,0:T(8,128)(2,1)S(1)}, bf16[1,7168,256]{2,1,0:T(8,128)(2,1)}, u32[]{:S(2)}) copy-start(bf16[1,7168,256]{2,1,0:T(8,128)(2,1)} %param.9) | copy-start | bytes 11010052
  68.8 3.3 %copy-start = (bf16[1,256,7168]{2,1,0:T(8,128)(2,1)S(1)}, bf16[1,256,7168]{2,1,0:T(8,128)(2,1)}, u32[]{:S(2)}) copy-start(bf16[1,256,7168]{2,1,0:T(8,128)(2,1)} %param.11) | copy-start | bytes 11010052
  74.5 4.0 %collective-permute-start.2 = (bf16[512,1792]{1,0:T(8,128)(2,1)S(1)}, bf16[512,1792]{1,0:T(8,128)(2,1)S(1)}, u32[]{:S(2)}, u32[]{:S(2)}) collective-permute-start(bf16[512,1792]{1,0:T(8,128)(2,1)S(1)} %down.3), channel_id=1, source_target_pairs={{0,1},{1,0},{2,3},{3,2},{4,5},{5,4},{6,7},{7,6},{8,9},{9,8},{10,11... | collective-permute-start | bytes 5505032 | tf_op jit(solution)/shard_map/ppermute | solution.py:21
  75.1 6.0 %collective-permute-start.1 = (bf16[512,1792]{1,0:T(8,128)(2,1)S(1)}, bf16[512,1792]{1,0:T(8,128)(2,1)S(1)}, u32[]{:S(2)}, u32[]{:S(2)}) collective-permute-start(bf16[512,1792]{1,0:T(8,128)(2,1)S(1)} %down.2), channel_id=1, source_target_pairs={{0,1},{1,0},{2,3},{3,2},{4,5},{5,4},{6,7},{7,6},{8,9},{9,8},{10,11... | collective-permute-start | bytes 5505032 | tf_op jit(solution)/shard_map/ppermute | solution.py:21
  83.8 1.8 %copy-start.1 = (bf16[512,3584]{1,0:T(8,128)(2,1)}, bf16[512,3584]{1,0:T(8,128)(2,1)S(1)}, u32[]{:S(2)}) copy-start(bf16[512,3584]{1,0:T(8,128)(2,1)S(1)} %down_add.1) | copy-start | bytes 11010052
  85.7 6.0 %copy-start.2 = (s32[32,8]{0,1:T(8,128)S(1)}, s32[32,8]{0,1:T(8,128)}, u32[]{:S(2)}) copy-start(s32[32,8]{0,1:T(8,128)} %param.8) | copy-start | bytes 3076
  85.7 6.1 %copy-start.3 = (f32[32,8]{0,1:T(8,128)S(1)}, f32[32,8]{0,1:T(8,128)}, u32[]{:S(2)}) copy-start(f32[32,8]{0,1:T(8,128)} %param.7) | copy-start | bytes 3076
  85.7 60.5 %all-to-all-start.1 = ((bf16[32,16,3584]{2,1,0:T(8,128)(2,1)}), bf16[32,16,3584]{2,1,0:T(8,128)(2,1)}, u32[]{:S(2)}, u32[]{:S(2)}) async-start(bf16[32,16,3584]{2,1,0:T(8,128)(2,1)} %bitcast.46), calls=%async_computation.1 | async-start | bytes 7340032 | tf_op jit(solution)/shard_map/all_to_all | solution.py:192

commit v3 on v2

v3 whole, which is shorter than its diff:
```python
import jax
import jax.numpy as jnp
from jax import lax
from jax.experimental import pallas as pl
from jax.experimental.pallas import tpu as pltpu
from jax.sharding import PartitionSpec as P


EXPERTS = 32
CAP = 8
MB = 2
TOK_MB = 16
INTERPRET = False
BF = jnp.bfloat16
F32 = jnp.float32


def dot(a, b):
    return jnp.dot(a, b, preferred_element_type=F32)


def other_core(a):
    return lax.ppermute(a, "tp", [(0, 1), (1, 0)])


def iota(shape, dim):
    return lax.broadcasted_iota(jnp.int32, shape, dim)


def bits(mask):
    return mask.astype(F32).astype(BF)


def place_body(micro, ids_t, tokens, out, placing):
    @pl.when(pl.program_id(0) == 0)
    def _():
        top, count = ids_t.shape
        rows = placing.shape[0]
        expert = iota((EXPERTS, count), 0)
        chosen = jnp.zeros((EXPERTS, count), F32)
        for k in range(top):
            chosen += (ids_t[k : k + 1, :] == expert).astype(F32)
        i, j = iota((count, count), 0), iota((count, count), 1)
        before = dot(chosen.astype(BF), bits((i // TOK_MB == j // TOK_MB) & (i < j)))
        target = jnp.where(chosen > 0.5, before, -1.0).astype(BF)
        of_row = bits(iota((rows, EXPERTS), 0) // CAP == iota((rows, EXPERTS), 1))
        target = dot(of_row, target)
        r, c = iota((rows, count), 0), iota((rows, count), 1)
        hit = (target == (r % CAP).astype(F32)) & (c // TOK_MB == micro)
        placing[...] = bits(hit)

    out[...] = dot(placing[...], tokens[...]).astype(BF)


def place(tokens, expert_ids, micro):
    count, width = tokens.shape
    rows = EXPERTS * CAP
    block = width // 4
    return pl.pallas_call(
        lambda *refs: place_body(micro, *refs),
        out_shape=jax.ShapeDtypeStruct((rows, width), BF),
        grid=(4,),
        in_specs=[
            pl.BlockSpec(expert_ids.shape[::-1], lambda i: (0, 0)),
            pl.BlockSpec((count, block), lambda i: (0, i)),
        ],
        out_specs=pl.BlockSpec((rows, block), lambda i: (0, i)),
        scratch_shapes=[pltpu.VMEM((rows, count), BF)],
        interpret=INTERPRET,
        name="place",
    )(jnp.transpose(expert_ids), tokens)


def mixing(gates, expert_ids):
    count = gates.shape[0]
    blocks = count // TOK_MB
    onehot = (expert_ids[:, :, None] == lax.iota(jnp.int32, EXPERTS)).astype(F32)
    chosen = jnp.sum(onehot, axis=1)
    weight = jnp.sum(onehot * gates[:, :, None], axis=1)
    earlier = (iota((TOK_MB, TOK_MB), 1) < iota((TOK_MB, TOK_MB), 0)).astype(F32)
    before = jnp.einsum("ts,bse->bte", earlier, chosen.reshape(blocks, TOK_MB, EXPERTS))
    target = jnp.where(chosen > 0.5, before.reshape(count, EXPERTS), -1.0)[:, :, None]
    column = iota((1, 1, blocks * CAP), 2)
    own = column // CAP == iota((count, 1, 1), 0) // TOK_MB
    hit = own & (target == (column % CAP).astype(F32))
    mix = jnp.where(hit, weight[:, :, None], 0.0).reshape(count, -1)
    high = lax.reduce_precision(mix, 8, 7)
    middle = lax.reduce_precision(mix - high, 8, 7)
    return jnp.concatenate([high, middle, mix - high - middle], axis=0).astype(BF)


def mix_body(first, mix, rows, out):
    total = dot(mix[...], rows[...])
    n = total.shape[0] // 3
    out[...] = (total[:n] + total[n : 2 * n] + total[2 * n :]).astype(BF)[None]


def mix_rows(mix, rows, first):
    slots, width = rows.shape
    count = mix.shape[0] // 3
    block = width // 4
    return pl.pallas_call(
        mix_body,
        out_shape=jax.ShapeDtypeStruct((4, count, block), BF),
        grid_spec=pltpu.PrefetchScalarGridSpec(
            num_scalar_prefetch=1,
            grid=(4,),
            in_specs=[
                pl.BlockSpec(mix.shape, lambda i, f: (0, 0)),
                pl.BlockSpec((slots, block), lambda i, f: (0, (i + f[0]) % 4)),
            ],
            out_specs=pl.BlockSpec((1, count, block), lambda i, f: (i, 0, 0)),
        ),
        compiler_params=pltpu.CompilerParams(vmem_limit_bytes=8 << 20),
        interpret=INTERPRET,
        name="mix",
    )(first, mix, rows)


def down_body(t, hidden, weight, out):
    out[...] = dot(hidden[...], weight[...]).astype(BF)


def down_add_body(t, hidden, weight, term, out):
    out[...] = (dot(hidden[...], weight[...]) + term[...].astype(F32)).astype(BF)


def down(hidden, weight, which, term=None):
    slots, inner = hidden.shape
    block = weight.shape[1] // 8
    piece = pl.BlockSpec((slots, block), lambda i, t: (0, i))
    ins = [
        pl.BlockSpec((slots, inner), lambda i, t: (0, 0)),
        pl.BlockSpec((inner, block), lambda i, t: (0, 2 * i + t[0])),
    ]
    return pl.pallas_call(
        down_body if term is None else down_add_body,
        out_shape=jax.ShapeDtypeStruct((slots, 4 * block), BF),
        grid_spec=pltpu.PrefetchScalarGridSpec(
            num_scalar_prefetch=1,
            grid=(4,),
            in_specs=ins if term is None else ins + [piece],
            out_specs=piece,
        ),
        compiler_params=pltpu.CompilerParams(vmem_limit_bytes=12 << 20),
        interpret=INTERPRET,
        name="down" if term is None else "down_add",
    )(which, hidden, weight, *(() if term is None else (term,)))


def layer(tokens, gates, expert_ids, gate_weight, up_weight, down_weight):
    downw = down_weight[0]
    t = lax.axis_index("tp").astype(jnp.int32)
    group = lax.axis_index("grp").astype(jnp.int32).reshape(1)
    which = t.reshape(1)
    count, width = tokens.shape[0] // MB, tokens.shape[1]
    slots = EXPERTS * CAP
    gate = gate_weight.reshape(2, width, -1)
    up = up_weight.reshape(2, width, -1)

    def half(weight, which):
        return lax.dynamic_index_in_dim(weight, which, 0, keepdims=False)

    def exchanged(x):
        x = x.reshape(EXPERTS, CAP, width)
        x = lax.all_to_all(x, "ep", split_axis=0, concat_axis=0, tiled=True)
        return x.reshape(slots, width)

    parts = [slice(m * count, (m + 1) * count) for m in range(MB)]
    results = []
    for m, part in enumerate(parts):
        sent = place(tokens, expert_ids, m)
        mix = mixing(gates[part], expert_ids[part])
        rows = exchanged(sent)
        peer = other_core(rows)
        g, u = dot(rows, half(gate, t)), dot(rows, half(up, t))
        g, u = g + dot(peer, half(gate, 1 - t)), u + dot(peer, half(up, 1 - t))
        hidden = (g * jax.nn.sigmoid(g) * u).astype(BF)
        term = other_core(down(hidden, downw, 1 - which))
        out = down(hidden, downw, which, term)
        back = exchanged(out)
        if m < MB - 1:
            blocks = mix_rows(mix, back, group)
            total = blocks[0].astype(F32)
            for d in (1, 2, 3):
                ring = [(i, (i + d) % 4) for i in range(4)]
                total += lax.ppermute(blocks[d], "grp", ring).astype(F32)
        else:
            blocks = mix_rows(mix, back, jnp.zeros_like(group))
            shares = lax.all_to_all(blocks, "grp", split_axis=0, concat_axis=0, tiled=True)
            total = jnp.sum(shares.astype(F32), axis=0)
        results.append(total.astype(BF))
    return jnp.concatenate(results, axis=0)


def solution(mesh):
    placed = (
        P("ep", "tp"),
        P("ep", None),
        P("ep", None),
        P("ep", None, ("grp", "tp")),
        P("ep", None, ("grp", "tp")),
        P("ep", ("grp", "tp"), None),
    )
    return jax.shard_map(
        layer, mesh=mesh, in_specs=placed, out_specs=P("ep", ("grp", "tp")), check_vma=False
    )
```

time: 171 us -> 166 us (0.971)
  blocking collectives: 71.1 us -> 0 us
  starting transfers between devices: 6.7 us -> 45.8 us
  Pallas kernels: 13.9 us -> 23.5 us
  local copies, waits for them, and re-layouts: 2.62 us -> 10.6 us
  waiting for transfers between devices: 58.5 us -> 65.7 us
  matrix products: 13.7 us -> 17.2 us
    all_to_all x2 -> x0, blocking collectives: 71.1 us -> none  [the longest x1 53.9 us: local(): rows = lax.all_to_all(sent, 'ep', split_axis=0, concat_axis=0, tiled=True)]
    all_to_all x1 -> x5, starting transfers between devices: 6 us -> 35 us  [the longest x4 27.1 us: exchanged(): x = lax.all_to_all(x, 'ep', split_axis=0, concat_axis=0, tiled=True)]
    ppermute x0 -> x3, starting transfers between devices: none -> 10.5 us  [layer(): total += lax.ppermute(blocks[d], 'grp', ring).astype(F32)]
    pallas_call x4 -> x6, Pallas kernels: 9.6 us -> 18.8 us  [the longest x4 10.7 us: down(): pl.pallas_call(down_body if term is None else down_add_body, out_shape=ja...]
    all_to_all x1 -> x5, waiting for transfers between devices: 52.6 us -> 61.7 us  [the longest x4 53.5 us: exchanged(): x = lax.all_to_all(x, 'ep', split_axis=0, concat_axis=0, tiled=True)]
    unnamed x14 -> x24, local copies, waits for them, and re-layouts: 2 us -> 9.36 us
    dot_general x4 -> x8, matrix products: 13.6 us -> 16.9 us  [dot(): return jnp.dot(a, b, preferred_element_type=F32)]
    ppermute x3 -> x4, waiting for transfers between devices: 5.94 us -> 3.99 us  [other_core(): return lax.ppermute(a, 'tp', [(0, 1), (1, 0)])]
  transfers between devices with their start and end apart: 4 -> 12, of which waited for: 3 -> 6; matrix products, arithmetic and copies ran while one was open for 5% -> 11% of each run, Pallas kernels for 0% -> 12%
where the time goes in v3:
time: 166 us; the launch traced here: 164 us
  waiting for transfers between devices  65.7 us (40%)
  starting transfers between devices  45.8 us (28%)
  Pallas kernels  23.5 us (14%)
  matrix products  17.2 us (10%)
  local copies, waits for them, and re-layouts  10.6 us (6%)
    all_to_all x4, waiting for transfers between devices, exchanged(): x = lax.all_to_all(x, 'ep', split_axis=0, concat_axis=0, tiled=True)  53.5 us
    all_to_all x4, starting transfers between devices, exchanged(): x = lax.all_to_all(x, 'ep', split_axis=0, concat_axis=0, tiled=True)  27.1 us
    dot_general x8, matrix products, dot(): return jnp.dot(a, b, preferred_element_type=F32)  16.9 us
    pallas_call x4, Pallas kernels, down(): pl.pallas_call(down_body if term is None else down_add_body, out_shape=ja...  10.7 us
    ppermute x3, starting transfers between devices, layer(): total += lax.ppermute(blocks[d], 'grp', ring).astype(F32)  10.5 us
    unnamed x24, local copies, waits for them, and re-layouts  9.36 us
    all_to_all x1, waiting for transfers between devices, layer(): lax.all_to_all(blocks, 'grp', split_axis=0, concat_axis=0, tiled=True)  8.24 us
    pallas_call x2, Pallas kernels, place(): pl.pallas_call(lambda *refs: place_body(micro, *refs), out_shape=jax.Shap...  8.07 us
  transfers between devices with their start and end apart: 12, of which 6 were waited for; matrix products, arithmetic and copies ran while one was open for 11% of the time, Pallas kernels for 12%

profile of v3, /device:TPU:2, one launch (start us, length us, event | category | flops | bytes accessed | tf_op | source)
XLA Modules:
  0.0 164.2 jit_solution(3709168006076728271)
XLA Ops:
  0.0 4.0 %place.2 = bf16[256,3584]{1,0:T(8,128)(2,1)} custom-call(s32[8,32]{1,0:T(8,128)} %bitcast.115, bf16[32,3584]{1,0:T(8,128)(2,1)} %refs_1_.3), custom_call_target="tpu_custom_call" | custom-call | tf_op jit(solution)/shard_map/place/pallas_call | solution.py:59
  4.0 9.0 %all-to-all-start = ((bf16[32,8,3584]{2,1,0:T(8,128)(2,1)}), bf16[32,8,3584]{2,1,0:T(8,128)(2,1)S(1)}, u32[]{:S(2)}, u32[]{:S(2)}) async-start(bf16[32,8,3584]{2,1,0:T(8,128)(2,1)} %bitcast.110), calls=%async_computation | async-start | bytes 3670016 | tf_op jit(solution)/shard_map/all_to_all | solution.py:166
  13.0 4.1 %place.3 = bf16[256,3584]{1,0:T(8,128)(2,1)} custom-call(s32[8,32]{1,0:T(8,128)} %bitcast.116, bf16[32,3584]{1,0:T(8,128)(2,1)} %refs_1_.3), custom_call_target="tpu_custom_call" | custom-call | tf_op jit(solution)/shard_map/place/pallas_call | solution.py:59
  17.1 21.3 %all-to-all-done = bf16[32,8,3584]{2,1,0:T(8,128)(2,1)S(1)} async-done(((bf16[32,8,3584]{2,1,0:T(8,128)(2,1)}), bf16[32,8,3584]{2,1,0:T(8,128)(2,1)S(1)}, u32[]{:S(2)}, u32[]{:S(2)}) %all-to-all-start) | async-done | bytes 1835040 | tf_op jit(solution)/shard_map/all_to_all | solution.py:166
  38.3 5.7 %all-to-all-start.2 = ((bf16[32,8,3584]{2,1,0:T(8,128)(2,1)}), bf16[32,8,3584]{2,1,0:T(8,128)(2,1)}, u32[]{:S(2)}, u32[]{:S(2)}) async-start(bf16[32,8,3584]{2,1,0:T(8,128)(2,1)} %bitcast.109), calls=%async_computation.2 | async-start | bytes 3670016 | tf_op jit(solution)/shard_map/all_to_all | solution.py:166
  44.1 2.3 %fusion.14 = f32[256,256]{1,0:T(8,128)S(1)} fusion(bf16[2,3584,256]{2,1,0:T(8,128)(2,1)} %bitcast.105, s32[]{:T(128)S(6)} %select_n.84, bf16[32,8,3584]{2,1,0:T(8,128)(2,1)S(1)} %all-to-all-done), kind=kOutput, calls=%fused_computation.14 | convolution fusion | flops 469762048 | bytes 3932164 | tf_op jit(solution)/shard_map/dot_general | solution.py:19
  46.4 0.3 copy-done.8
  46.7 0.6 fusion.6
  47.3 1.4 copy-done.6
  48.7 2.1 %fusion.24 = f32[256,256]{1,0:T(8,128)S(1)} fusion(f32[256,256]{1,0:T(8,128)S(1)} %fusion.14, bf16[256,3584]{1,0:T(8,128)(2,1)} %collective-permute-done, bf16[2,3584,256]{2,1,0:T(8,128)(2,1)S(1)} %bitcast.107, s32[]{:T(128)S(6)} %select_n.85), kind=kOutput, calls=%fused_computation.24 | convolution fusion | flops 469827584 | bytes 4194308 | tf_op jit(solution)/shard_map/dot_general | solution.py:19
  50.9 2.3 %multiply_convert_fusion.1.hidden = bf16[256,256]{1,0:T(8,128)(2,1)S(1)} fusion(f32[256,256]{1,0:T(8,128)S(1)} %fusion.24, f32[256,256]{1,0:T(8,128)S(1)} %fusion.6, bf16[256,3584]{1,0:T(8,128)(2,1)} %collective-permute-done, bf16[2,3584,256]{2,1,0:T(8,128)(2,1)S(1)} %bitcast.112, s32[]{:T(128)S(6)} %select_n.85), kind=kOutput, calls=%fused_computation.33 | convolution fusion | flops 470220800 | bytes 4325380 | tf_op jit(solution)/shard_map/dot_general | solution.py:19
  53.2 0.3 copy-done
  53.5 1.6 down.2
  55.0 0.3 collective-permute-start.1
  55.3 16.3 %all-to-all-done.2 = bf16[32,8,3584]{2,1,0:T(8,128)(2,1)} async-done(((bf16[32,8,3584]{2,1,0:T(8,128)(2,1)}), bf16[32,8,3584]{2,1,0:T(8,128)(2,1)}, u32[]{:S(2)}, u32[]{:S(2)}) %all-to-all-start.2) | async-done | bytes 1835040 | tf_op jit(solution)/shard_map/all_to_all | solution.py:166
  71.6 2.0 %copy-done.1 = bf16[1,256,7168]{2,1,0:T(8,128)(2,1)S(1)} copy-done((bf16[1,256,7168]{2,1,0:T(8,128)(2,1)S(1)}, bf16[1,256,7168]{2,1,0:T(8,128)(2,1)}, u32[]{:S(2)}) %copy-start.1) | copy-done | bytes 3670040
  73.7 3.2 %down_add.2 = bf16[256,3584]{1,0:T(8,128)(2,1)S(1)} custom-call(s32[1]{0:T(128)} %bitcast.7.t, bf16[256,256]{1,0:T(8,128)(2,1)S(1)} %multiply_convert_fusion.1.hidden, bf16[256,7168]{1,0:T(8,128)(2,1)S(1)} %bitcast.98, bf16[256,3584]{1,0:T(8,128)(2,1)} %collective-permute-done.1.term), custom_call_target="tpu_custom_call" | custom-call | tf_op jit(solution)/shard_map/down_add/pallas_call | solution.py:136
  76.9 1.3 copy-done.5
  78.2 6.3 %all-to-all-start.1 = ((bf16[32,8,3584]{2,1,0:T(8,128)(2,1)}), bf16[32,8,3584]{2,1,0:T(8,128)(2,1)S(1)}, u32[]{:S(2)}, u32[]{:S(2)}) async-start(bf16[32,8,3584]{2,1,0:T(8,128)(2,1)} %bitcast.103), calls=%async_computation.1 | async-start | bytes 3670016 | tf_op jit(solution)/shard_map/all_to_all | solution.py:166
  84.5 2.8 %fusion.12 = f32[256,256]{1,0:T(8,128)S(1)} fusion(bf16[2,3584,256]{2,1,0:T(8,128)(2,1)} %bitcast.106, s32[]{:T(128)S(6)} %select_n.84, bf16[32,8,3584]{2,1,0:T(8,128)(2,1)} %all-to-all-done.2), kind=kOutput, calls=%fused_computation.12 | convolution fusion | flops 469762048 | bytes 3932164 | tf_op jit(solution)/shard_map/dot_general | solution.py:19
  87.3 0.3 copy-done.9
  87.6 2.3 %fusion.4 = f32[256,256]{1,0:T(8,128)S(1)} fusion(bf16[2,3584,256]{2,1,0:T(8,128)(2,1)S(1)} %bitcast.113, s32[]{:T(128)S(6)} %select_n.84, bf16[32,8,3584]{2,1,0:T(8,128)(2,1)} %all-to-all-done.2), kind=kOutput, calls=%fused_computation.4 | convolution fusion | flops 469762048 | bytes 3932164 | tf_op jit(solution)/shard_map/dot_general | solution.py:19
  89.9 0.3 copy-done.7
  90.2 2.1 %fusion.27 = f32[256,256]{1,0:T(8,128)S(1)} fusion(f32[256,256]{1,0:T(8,128)S(1)} %fusion.12, bf16[256,3584]{1,0:T(8,128)(2,1)} %collective-permute-done.5, bf16[2,3584,256]{2,1,0:T(8,128)(2,1)S(1)} %bitcast.108, s32[]{:T(128)S(6)} %select_n.85), kind=kOutput, calls=%fused_computation.25 | convolution fusion | flops 469827584 | bytes 4194308 | tf_op jit(solution)/shard_map/dot_general | solution.py:19
  92.4 2.3 %multiply_convert_fusion.hidden = bf16[256,256]{1,0:T(8,128)(2,1)S(1)} fusion(f32[256,256]{1,0:T(8,128)S(1)} %fusion.27, f32[256,256]{1,0:T(8,128)S(1)} %fusion.4, bf16[256,3584]{1,0:T(8,128)(2,1)} %collective-permute-done.5, bf16[2,3584,256]{2,1,0:T(8,128)(2,1)S(1)} %bitcast.114, s32[]{:T(128)S(6)} %select_n.85), kind=kOutput, calls=%fused_computation.32 | convolution fusion | flops 470220800 | bytes 4325380 | tf_op jit(solution)/shard_map/dot_general | solution.py:19
  94.7 0.3 copy-done.2
  95.0 2.7 %down.3 = bf16[256,3584]{1,0:T(8,128)(2,1)} custom-call(s32[1]{0:T(128)S(6)} %sub.43.t, bf16[256,256]{1,0:T(8,128)(2,1)S(1)} %multiply_convert_fusion.hidden, bf16[256,7168]{1,0:T(8,128)(2,1)S(1)} %bitcast.99), custom_call_target="tpu_custom_call" | custom-call | tf_op jit(solution)/shard_map/down/pallas_call | solution.py:136
  97.8 4.0 %collective-permute-done.6.term = bf16[256,3584]{1,0:T(8,128)(2,1)} collective-permute-done((bf16[256,3584]{1,0:T(8,128)(2,1)}, bf16[256,3584]{1,0:T(8,128)(2,1)}, u32[]{:S(2)}, u32[]{:S(2)}) %collective-permute-start.6) | collective-permute-done | bytes 1835040 | tf_op jit(solution)/shard_map/ppermute | solution.py:23
  101.7 2.0 %copy-done.3 = bf16[1,256,7168]{2,1,0:T(8,128)(2,1)S(1)} copy-done((bf16[1,256,7168]{2,1,0:T(8,128)(2,1)S(1)}, bf16[1,256,7168]{2,1,0:T(8,128)(2,1)}, u32[]{:S(2)}) %copy-start.3) | copy-done | bytes 3670040
  103.8 3.2 %down_add.3 = bf16[256,3584]{1,0:T(8,128)(2,1)S(1)} custom-call(s32[1]{0:T(128)} %bitcast.7.t, bf16[256,256]{1,0:T(8,128)(2,1)S(1)} %multiply_convert_fusion.hidden, bf16[256,7168]{1,0:T(8,128)(2,1)S(1)} %bitcast.100, bf16[256,3584]{1,0:T(8,128)(2,1)} %collective-permute-done.6.term), custom_call_target="tpu_custom_call" | custom-call | tf_op jit(solution)/shard_map/down_add/pallas_call | solution.py:136
  107.0 1.2 copy-done.4
  108.3 3.0 %all-to-all-done.1 = bf16[32,8,3584]{2,1,0:T(8,128)(2,1)S(1)} async-done(((bf16[32,8,3584]{2,1,0:T(8,128)(2,1)}), bf16[32,8,3584]{2,1,0:T(8,128)(2,1)S(1)}, u32[]{:S(2)}, u32[]{:S(2)}) %all-to-all-start.1) | async-done | bytes 1835040 | tf_op jit(solution)/shard_map/all_to_all | solution.py:166
  111.3 6.1 %all-to-all-start.3 = ((bf16[32,8,3584]{2,1,0:T(8,128)(2,1)}), bf16[32,8,3584]{2,1,0:T(8,128)(2,1)}, u32[]{:S(2)}, u32[]{:S(2)}) async-start(bf16[32,8,3584]{2,1,0:T(8,128)(2,1)} %bitcast.102), calls=%async_computation.3 | async-start | bytes 3670016 | tf_op jit(solution)/shard_map/all_to_all | solution.py:166
  117.6 0.1 convert_reduce_fusion.1
  117.7 0.1 fusion.37
  118.1 0.1 convert_reduce_fusion
  118.3 0.1 fusion.36
  118.9 0.1 broadcast_compare_fusion
  119.1 0.1 eq.109
  119.2 1.1 mix.2
  120.3 3.3 %collective-permute-start.2 = (bf16[16,896]{1,0:T(8,128)(2,1)S(1)}, bf16[16,896]{1,0:T(8,128)(2,1)S(1)}, u32[]{:S(2)}, u32[]{:S(2)}) collective-permute-start(bf16[16,896]{1,0:T(8,128)(2,1)S(1)} %get-tuple-element.13), channel_id=1, source_target_pairs={{0,64},{64,128},{128,192},{192,0},{1,65},{65,129},{129,193},{193,1... | collective-permute-start | bytes 86024 | tf_op jit(solution)/shard_map/ppermute | solution.py:187
  123.7 4.5 %collective-permute-start.3 = (bf16[16,896]{1,0:T(8,128)(2,1)S(1)}, bf16[16,896]{1,0:T(8,128)(2,1)S(1)}, u32[]{:S(2)}, u32[]{:S(2)}) collective-permute-start(bf16[16,896]{1,0:T(8,128)(2,1)S(1)} %get-tuple-element.15), channel_id=1, source_target_pairs={{0,128},{64,192},{128,0},{192,64},{1,129},{65,193},{129,1},{193,65... | collective-permute-start | bytes 86024 | tf_op jit(solution)/shard_map/ppermute | solution.py:187
  128.2 2.7 %collective-permute-start.4 = (bf16[16,896]{1,0:T(8,128)(2,1)S(1)}, bf16[16,896]{1,0:T(8,128)(2,1)S(1)}, u32[]{:S(2)}, u32[]{:S(2)}) collective-permute-start(bf16[16,896]{1,0:T(8,128)(2,1)S(1)} %get-tuple-element.14), channel_id=1, source_target_pairs={{0,192},{64,0},{128,64},{192,128},{1,193},{65,1},{129,65},{193,129... | collective-permute-start | bytes 86024 | tf_op jit(solution)/shard_map/ppermute | solution.py:187
  130.8 12.8 %all-to-all-done.3 = bf16[32,8,3584]{2,1,0:T(8,128)(2,1)} async-done(((bf16[32,8,3584]{2,1,0:T(8,128)(2,1)}), bf16[32,8,3584]{2,1,0:T(8,128)(2,1)}, u32[]{:S(2)}, u32[]{:S(2)}) %all-to-all-start.3) | async-done | bytes 1835040 | tf_op jit(solution)/shard_map/all_to_all | solution.py:166
  143.7 3.7 %mix.3 = bf16[4,16,896]{2,1,0:T(8,128)(2,1)} custom-call(s32[1]{0:T(128)} %constant.98.clone.1.first, bf16[48,256]{1,0:T(8,128)(2,1)S(1)} %pad_maximum_fusion.2.mix, bf16[256,3584]{1,0:T(8,128)(2,1)} %bitcast.32.rows), custom_call_target="tpu_custom_call" | custom-call | tf_op jit(solution)/shard_map/mix/pallas_call | solution.py:102
  147.4 7.9 %all-to-all-start.4 = ((bf16[4,16,896]{2,1,0:T(8,128)(2,1)}), bf16[4,16,896]{2,1,0:T(8,128)(2,1)S(1)}, u32[]{:S(2)}, u32[]{:S(2)}) async-start(bf16[4,16,896]{2,1,0:T(8,128)(2,1)} %mix.3), calls=%async_computation.4 | async-start | bytes 229376 | tf_op jit(solution)/shard_map/all_to_all | solution.py:190
  155.3 8.2 %all-to-all-done.4 = bf16[4,16,896]{2,1,0:T(8,128)(2,1)S(1)} async-done(((bf16[4,16,896]{2,1,0:T(8,128)(2,1)}), bf16[4,16,896]{2,1,0:T(8,128)(2,1)S(1)}, u32[]{:S(2)}, u32[]{:S(2)}) %all-to-all-start.4) | async-done | bytes 114720 | tf_op jit(solution)/shard_map/all_to_all | solution.py:190
  163.6 0.6 pad_maximum_fusion
  (54 shorter events, 1.3 us)
Async XLA Ops:
  4.0 34.3 %all-to-all-start = ((bf16[32,8,3584]{2,1,0:T(8,128)(2,1)}), bf16[32,8,3584]{2,1,0:T(8,128)(2,1)S(1)}, u32[]{:S(2)}, u32[]{:S(2)}) async-start(bf16[32,8,3584]{2,1,0:T(8,128)(2,1)} %bitcast.110), calls=%async_computation | async-start | bytes 3670016 | tf_op jit(solution)/shard_map/all_to_all | solution.py:166
  38.3 9.0 %collective-permute-start = (bf16[256,3584]{1,0:T(8,128)(2,1)S(1)}, bf16[256,3584]{1,0:T(8,128)(2,1)}, u32[]{:S(2)}, u32[]{:S(2)}) collective-permute-start(bf16[256,3584]{1,0:T(8,128)(2,1)S(1)} %bitcast.104), channel_id=1, source_target_pairs={{0,1},{1,0},{2,3},{3,2},{4,5},{5,4},{6,7},{7,6},{8,9},{9,8},{10,11... | collective-permute-start | bytes 5505032 | tf_op jit(solution)/shard_map/ppermute | solution.py:23
  38.3 33.3 %all-to-all-start.2 = ((bf16[32,8,3584]{2,1,0:T(8,128)(2,1)}), bf16[32,8,3584]{2,1,0:T(8,128)(2,1)}, u32[]{:S(2)}, u32[]{:S(2)}) async-start(bf16[32,8,3584]{2,1,0:T(8,128)(2,1)} %bitcast.109), calls=%async_computation.2 | async-start | bytes 3670016 | tf_op jit(solution)/shard_map/all_to_all | solution.py:166
  44.1 2.6 %copy-start.8 = (bf16[1,7168,256]{2,1,0:T(8,128)(2,1)S(1)}, bf16[1,7168,256]{2,1,0:T(8,128)(2,1)}, u32[]{:S(2)}) copy-start(bf16[1,7168,256]{2,1,0:T(8,128)(2,1)} %param.10) | copy-start | bytes 11010052
  46.7 2.0 %copy-start.6 = (bf16[1,7168,256]{2,1,0:T(8,128)(2,1)S(1)}, bf16[1,7168,256]{2,1,0:T(8,128)(2,1)}, u32[]{:S(2)}) copy-start(bf16[1,7168,256]{2,1,0:T(8,128)(2,1)} %param.9) | copy-start | bytes 11010052
  50.9 2.6 %copy-start = (bf16[1,256,7168]{2,1,0:T(8,128)(2,1)S(1)}, bf16[1,256,7168]{2,1,0:T(8,128)(2,1)}, u32[]{:S(2)}) copy-start(bf16[1,256,7168]{2,1,0:T(8,128)(2,1)} %param.11) | copy-start | bytes 11010052
  55.0 16.6 %collective-permute-start.1 = (bf16[256,3584]{1,0:T(8,128)(2,1)S(1)}, bf16[256,3584]{1,0:T(8,128)(2,1)}, u32[]{:S(2)}, u32[]{:S(2)}) collective-permute-start(bf16[256,3584]{1,0:T(8,128)(2,1)S(1)} %down.2), channel_id=1, source_target_pairs={{0,1},{1,0},{2,3},{3,2},{4,5},{5,4},{6,7},{7,6},{8,9},{9,8},{10,11... | collective-permute-start | bytes 5505032 | tf_op jit(solution)/shard_map/ppermute | solution.py:23
  71.6 18.3 %collective-permute-start.5 = (bf16[256,3584]{1,0:T(8,128)(2,1)}, bf16[256,3584]{1,0:T(8,128)(2,1)}, u32[]{:S(2)}, u32[]{:S(2)}) collective-permute-start(bf16[256,3584]{1,0:T(8,128)(2,1)} %bitcast.30), channel_id=1, source_target_pairs={{0,1},{1,0},{2,3},{3,2},{4,5},{5,4},{6,7},{7,6},{8,9},{9,8},{10,11... | collective-permute-start | bytes 5505032 | tf_op jit(solution)/shard_map/ppermute | solution.py:23
  71.6 2.0 %copy-start.1 = (bf16[1,256,7168]{2,1,0:T(8,128)(2,1)S(1)}, bf16[1,256,7168]{2,1,0:T(8,128)(2,1)}, u32[]{:S(2)}) copy-start(bf16[1,256,7168]{2,1,0:T(8,128)(2,1)} %param.11) | copy-start | bytes 11010052
  76.9 1.3 copy-start.5
  78.2 33.1 %all-to-all-start.1 = ((bf16[32,8,3584]{2,1,0:T(8,128)(2,1)}), bf16[32,8,3584]{2,1,0:T(8,128)(2,1)S(1)}, u32[]{:S(2)}, u32[]{:S(2)}) async-start(bf16[32,8,3584]{2,1,0:T(8,128)(2,1)} %bitcast.103), calls=%async_computation.1 | async-start | bytes 3670016 | tf_op jit(solution)/shard_map/all_to_all | solution.py:166
  84.5 3.1 %copy-start.9 = (bf16[1,7168,256]{2,1,0:T(8,128)(2,1)S(1)}, bf16[1,7168,256]{2,1,0:T(8,128)(2,1)}, u32[]{:S(2)}) copy-start(bf16[1,7168,256]{2,1,0:T(8,128)(2,1)} %param.10) | copy-start | bytes 11010052
  87.6 2.6 %copy-start.7 = (bf16[1,7168,256]{2,1,0:T(8,128)(2,1)S(1)}, bf16[1,7168,256]{2,1,0:T(8,128)(2,1)}, u32[]{:S(2)}) copy-start(bf16[1,7168,256]{2,1,0:T(8,128)(2,1)} %param.9) | copy-start | bytes 11010052
  92.4 2.6 %copy-start.2 = (bf16[1,256,7168]{2,1,0:T(8,128)(2,1)S(1)}, bf16[1,256,7168]{2,1,0:T(8,128)(2,1)}, u32[]{:S(2)}) copy-start(bf16[1,256,7168]{2,1,0:T(8,128)(2,1)} %param.11) | copy-start | bytes 11010052
  95.0 2.7 %copy-start.10 = (s32[32,8]{0,1:T(8,128)S(1)}, s32[32,8]{0,1:T(8,128)}, u32[]{:S(2)}) copy-start(s32[32,8]{0,1:T(8,128)} %param.8) | copy-start | bytes 3076
  97.6 4.1 %collective-permute-start.6 = (bf16[256,3584]{1,0:T(8,128)(2,1)}, bf16[256,3584]{1,0:T(8,128)(2,1)}, u32[]{:S(2)}, u32[]{:S(2)}) collective-permute-start(bf16[256,3584]{1,0:T(8,128)(2,1)} %down.3), channel_id=1, source_target_pairs={{0,1},{1,0},{2,3},{3,2},{4,5},{5,4},{6,7},{7,6},{8,9},{9,8},{10,11... | collective-permute-start | bytes 5505032 | tf_op jit(solution)/shard_map/ppermute | solution.py:23
  101.7 2.0 %copy-start.3 = (bf16[1,256,7168]{2,1,0:T(8,128)(2,1)S(1)}, bf16[1,256,7168]{2,1,0:T(8,128)(2,1)}, u32[]{:S(2)}) copy-start(bf16[1,256,7168]{2,1,0:T(8,128)(2,1)} %param.11) | copy-start | bytes 11010052
  107.0 1.2 copy-start.4
  111.3 6.1 %copy-start.11 = (f32[32,8]{0,1:T(8,128)S(1)}, f32[32,8]{0,1:T(8,128)}, u32[]{:S(2)}) copy-start(f32[32,8]{0,1:T(8,128)} %param.7) | copy-start | bytes 3076
  111.3 32.4 %all-to-all-start.3 = ((bf16[32,8,3584]{2,1,0:T(8,128)(2,1)}), bf16[32,8,3584]{2,1,0:T(8,128)(2,1)}, u32[]{:S(2)}, u32[]{:S(2)}) async-start(bf16[32,8,3584]{2,1,0:T(8,128)(2,1)} %bitcast.102), calls=%async_computation.3 | async-start | bytes 3670016 | tf_op jit(solution)/shard_map/all_to_all | solution.py:166
  120.3 34.9 %collective-permute-start.2 = (bf16[16,896]{1,0:T(8,128)(2,1)S(1)}, bf16[16,896]{1,0:T(8,128)(2,1)S(1)}, u32[]{:S(2)}, u32[]{:S(2)}) collective-permute-start(bf16[16,896]{1,0:T(8,128)(2,1)S(1)} %get-tuple-element.13), channel_id=1, source_target_pairs={{0,64},{64,128},{128,192},{192,0},{1,65},{65,129},{129,193},{193,1... | collective-permute-start | bytes 86024 | tf_op jit(solution)/shard_map/ppermute | solution.py:187
  123.7 31.6 %collective-permute-start.3 = (bf16[16,896]{1,0:T(8,128)(2,1)S(1)}, bf16[16,896]{1,0:T(8,128)(2,1)S(1)}, u32[]{:S(2)}, u32[]{:S(2)}) collective-permute-start(bf16[16,896]{1,0:T(8,128)(2,1)S(1)} %get-tuple-element.15), channel_id=1, source_target_pairs={{0,128},{64,192},{128,0},{192,64},{1,129},{65,193},{129,1},{193,65... | collective-permute-start | bytes 86024 | tf_op jit(solution)/shard_map/ppermute | solution.py:187
  128.2 27.1 %collective-permute-start.4 = (bf16[16,896]{1,0:T(8,128)(2,1)S(1)}, bf16[16,896]{1,0:T(8,128)(2,1)S(1)}, u32[]{:S(2)}, u32[]{:S(2)}) collective-permute-start(bf16[16,896]{1,0:T(8,128)(2,1)S(1)} %get-tuple-element.14), channel_id=1, source_target_pairs={{0,192},{64,0},{128,64},{192,128},{1,193},{65,1},{129,65},{193,129... | collective-permute-start | bytes 86024 | tf_op jit(solution)/shard_map/ppermute | solution.py:187
  147.4 16.2 %all-to-all-start.4 = ((bf16[4,16,896]{2,1,0:T(8,128)(2,1)}), bf16[4,16,896]{2,1,0:T(8,128)(2,1)S(1)}, u32[]{:S(2)}, u32[]{:S(2)}) async-start(bf16[4,16,896]{2,1,0:T(8,128)(2,1)} %mix.3), calls=%async_computation.4 | async-start | bytes 229376 | tf_op jit(solution)/shard_map/all_to_all | solution.py:190

commit v4 on v3

v4 whole, which is shorter than its diff:
```python
import jax
import jax.numpy as jnp
from jax import lax
from jax.experimental import pallas as pl
from jax.experimental.pallas import tpu as pltpu
from jax.sharding import Mesh
from jax.sharding import PartitionSpec as P


EXPERTS = 16
CAP = 8
TOK_MB = 16
INTERPRET = False
BF = jnp.bfloat16
F32 = jnp.float32


def dot(a, b):
    return jnp.dot(a, b, preferred_element_type=F32)


def other_core(a):
    return lax.ppermute(a, "tp", [(0, 1), (1, 0)])


def iota(shape, dim):
    return lax.broadcasted_iota(jnp.int32, shape, dim)


def bits(mask):
    return mask.astype(F32).astype(BF)


def place_body(plane, ids_t, tokens, out, placing):
    @pl.when(pl.program_id(0) == 0)
    def _():
        top, count = ids_t.shape
        rows = placing.shape[0]
        per = rows // EXPERTS
        expert = 2 * iota((EXPERTS, count), 0) + plane[0]
        chosen = jnp.zeros((EXPERTS, count), F32)
        for k in range(top):
            chosen += (ids_t[k : k + 1, :] == expert).astype(F32)
        i, j = iota((count, count), 0), iota((count, count), 1)
        before = dot(chosen.astype(BF), bits((i // TOK_MB == j // TOK_MB) & (i < j)))
        target = jnp.where(chosen > 0.5, before, -1.0).astype(BF)
        of_row = bits(iota((rows, EXPERTS), 0) // per == iota((rows, EXPERTS), 1))
        target = dot(of_row, target)
        r, c = iota((rows, count), 0), iota((rows, count), 1)
        hit = (target == (r % CAP).astype(F32)) & (c // TOK_MB == r % per // CAP)
        placing[...] = bits(hit)

    out[...] = dot(placing[...], tokens[...]).astype(BF)


def place(tokens, ids, plane):
    count, width = tokens.shape
    rows = EXPERTS * (count // TOK_MB) * CAP
    block = width // 4
    return pl.pallas_call(
        place_body,
        out_shape=jax.ShapeDtypeStruct((rows, width), BF),
        grid_spec=pltpu.PrefetchScalarGridSpec(
            num_scalar_prefetch=1,
            grid=(4,),
            in_specs=[
                pl.BlockSpec(ids.shape[::-1], lambda i, p: (0, 0)),
                pl.BlockSpec((count, block), lambda i, p: (0, i)),
            ],
            out_specs=pl.BlockSpec((rows, block), lambda i, p: (0, i)),
            scratch_shapes=[pltpu.VMEM((rows, count), BF)],
        ),
        interpret=INTERPRET,
        name="place",
    )(plane, jnp.transpose(ids), tokens)


def mixing(gates, ids, plane):
    count = gates.shape[0]
    blocks = count // TOK_MB
    onehot = (ids[:, :, None] == 2 * lax.iota(jnp.int32, EXPERTS) + plane).astype(F32)
    chosen = jnp.sum(onehot, axis=1)
    weight = jnp.sum(onehot * gates[:, :, None], axis=1)
    earlier = (iota((TOK_MB, TOK_MB), 1) < iota((TOK_MB, TOK_MB), 0)).astype(F32)
    before = jnp.einsum("ts,bse->bte", earlier, chosen.reshape(blocks, TOK_MB, EXPERTS))
    target = jnp.where(chosen > 0.5, before.reshape(count, EXPERTS), -1.0)[:, :, None]
    column = iota((1, 1, blocks * CAP), 2)
    own = column // CAP == iota((count, 1, 1), 0) // TOK_MB
    hit = own & (target == (column % CAP).astype(F32))
    mix = jnp.where(hit, weight[:, :, None], 0.0).reshape(count, -1)
    high = lax.reduce_precision(mix, 8, 7)
    middle = lax.reduce_precision(mix - high, 8, 7)
    return jnp.concatenate([high, middle, mix - high - middle], axis=0).astype(BF)


def mixed(mix, rows):
    total = dot(mix[...], rows[...])
    n = total.shape[0] // 3
    return (total[:n] + total[n : 2 * n] + total[2 * n :]).astype(BF)


def mix_body(plane, mix, rows, out):
    out[0] = mixed(mix, rows)


def mix_both_body(plane, mix, rows, first, out):
    out[0, plane[0]] = first[0]
    out[0, 1 - plane[0]] = mixed(mix, rows)


def mix_rows(mix, rows, plane, first=None):
    slots, width = rows.shape
    count = mix.shape[0] // 3
    block = width // 4
    one = pl.BlockSpec((1, count, block), lambda i, p: (i, 0, 0))
    ins = [
        pl.BlockSpec(mix.shape, lambda i, p: (0, 0)),
        pl.BlockSpec((slots, block), lambda i, p: (0, i)),
    ]
    if first is None:
        body, shape, spec, args = mix_body, (4, count, block), one, ()
    else:
        body, shape, args = mix_both_body, (4, 2, count, block), (first,)
        spec = pl.BlockSpec((1, 2, count, block), lambda i, p: (i, 0, 0, 0))
        ins.append(one)
    return pl.pallas_call(
        body,
        out_shape=jax.ShapeDtypeStruct(shape, BF),
        grid_spec=pltpu.PrefetchScalarGridSpec(
            num_scalar_prefetch=1, grid=(4,), in_specs=ins, out_specs=spec
        ),
        compiler_params=pltpu.CompilerParams(vmem_limit_bytes=8 << 20),
        interpret=INTERPRET,
        name="mix",
    )(plane, mix, rows, *args)


def down_body(t, hidden, weight, out):
    out[...] = dot(hidden[...], weight[...]).astype(BF)


def down_add_body(t, hidden, weight, term, out):
    out[...] = (dot(hidden[...], weight[...]) + term[...].astype(F32)).astype(BF)


def down(hidden, weight, which, term=None):
    slots, inner = hidden.shape
    block = weight.shape[1] // 8
    piece = pl.BlockSpec((slots, block), lambda i, t: (0, i))
    ins = [
        pl.BlockSpec((slots, inner), lambda i, t: (0, 0)),
        pl.BlockSpec((inner, block), lambda i, t: (0, 2 * i + t[0])),
    ]
    return pl.pallas_call(
        down_body if term is None else down_add_body,
        out_shape=jax.ShapeDtypeStruct((slots, 4 * block), BF),
        grid_spec=pltpu.PrefetchScalarGridSpec(
            num_scalar_prefetch=1,
            grid=(4,),
            in_specs=ins if term is None else ins + [piece],
            out_specs=piece,
        ),
        compiler_params=pltpu.CompilerParams(vmem_limit_bytes=12 << 20),
        interpret=INTERPRET,
        name="down" if term is None else "down_add",
    )(which, hidden, weight, *(() if term is None else (term,)))


def layer(tokens, gates, expert_ids, gate_weight, up_weight, down_weight):
    downw = down_weight[0]
    t = lax.axis_index("tp").astype(jnp.int32)
    plane = lax.axis_index("zl").astype(jnp.int32).reshape(1)
    which = t.reshape(1)
    width = tokens.shape[1]
    gate = gate_weight.reshape(2, width, -1)
    up = up_weight.reshape(2, width, -1)

    def half(weight, which):
        return lax.dynamic_index_in_dim(weight, which, 0, keepdims=False)

    def other_plane(x):
        return lax.ppermute(x, "zl", [(0, 1), (1, 0)])

    def exchanged(x):
        shape = x.shape
        x = x.reshape(EXPERTS, -1, width)
        x = lax.all_to_all(x, ("y", "x"), split_axis=0, concat_axis=0, tiled=True)
        return x.reshape(shape)

    choice = other_plane(jnp.concatenate([expert_ids.astype(F32), gates], axis=1))
    top = expert_ids.shape[1]
    sources = [
        (tokens, expert_ids, gates),
        (other_plane(tokens), choice[:, :top].astype(jnp.int32), choice[:, top:]),
    ]
    blocks = None
    for source, ids, weights in sources:
        sent = place(source, ids, plane)
        mix = mixing(weights, ids, plane)
        rows = exchanged(sent)
        peer = other_core(rows)
        g, u = dot(rows, half(gate, t)), dot(rows, half(up, t))
        g, u = g + dot(peer, half(gate, 1 - t)), u + dot(peer, half(up, 1 - t))
        hidden = (g * jax.nn.sigmoid(g) * u).astype(BF)
        term = other_core(down(hidden, downw, 1 - which))
        out = down(hidden, downw, which, term)
        back = exchanged(out)
        blocks = mix_rows(mix, back, plane, blocks)
    pieces = blocks.reshape(8, *blocks.shape[2:])
    shares = lax.all_to_all(pieces, ("grp", "zl"), split_axis=0, concat_axis=0, tiled=True)
    return jnp.sum(shares.astype(F32), axis=0).astype(BF)


def solution(mesh):
    fine = Mesh(mesh.devices.reshape(4, 4, 4, 2, 2), ("grp", "y", "x", "zl", "tp"))
    ep = ("y", "x", "zl")
    placed = (
        P(ep, "tp"),
        P(ep, None),
        P(ep, None),
        P(ep, None, ("grp", "tp")),
        P(ep, None, ("grp", "tp")),
        P(ep, ("grp", "tp"), None),
    )
    return jax.shard_map(
        layer, mesh=fine, in_specs=placed, out_specs=P(ep, ("grp", "tp")), check_vma=False
    )
```

time: 166 us -> 189 us (1.14)
  blocking collectives: 0 us -> 23 us
  waiting for transfers between devices: 65.7 us -> 81.9 us
  starting transfers between devices: 45.8 us -> 34 us
  local copies, waits for them, and re-layouts: 10.6 us -> 8.05 us
  Pallas kernels: 23.5 us -> 21.2 us
    all_to_all x0 -> x1, blocking collectives: none -> 23 us  [layer(): lax.all_to_all(pieces, ('grp', 'zl'), split_axis=0, concat_axis=0, tiled=...]
    all_to_all x5 -> x4, waiting for transfers between devices: 61.7 us -> 76.9 us  [exchanged(): x = lax.all_to_all(x, ('y', 'x'), split_axis=0, concat_axis=0, tiled=True)]
    ppermute x3 -> x2, starting transfers between devices: 10.5 us -> 2.2 us  [other_plane(): return lax.ppermute(x, 'zl', [(0, 1), (1, 0)])]
    ppermute x3 -> x2, waiting for transfers between devices: 0.01 us -> 5 us  [other_plane(): return lax.ppermute(x, 'zl', [(0, 1), (1, 0)])]
    ppermute x4, waiting for transfers between devices: 3.99 us -> 0.01 us  [other_core(): return lax.ppermute(a, 'tp', [(0, 1), (1, 0)])]
    all_to_all x5 -> x4, starting transfers between devices: 35 us -> 31.1 us  [exchanged(): x = lax.all_to_all(x, ('y', 'x'), split_axis=0, concat_axis=0, tiled=True)]
    unnamed x24 -> x20, local copies, waits for them, and re-layouts: 9.36 us -> 7.2 us
  transfers between devices with their start and end apart: 12 -> 10, of which waited for: 6 -> 5; matrix products, arithmetic and copies ran while one was open for 11% -> 10% of each run, Pallas kernels for 12% -> 8%
where the time goes in v4:
time: 189 us; the launch traced here: 186 us
  waiting for transfers between devices  81.9 us (43%)
  starting transfers between devices  34 us (18%)
  blocking collectives  23 us (12%)
  Pallas kernels  21.2 us (11%)
  matrix products  16.2 us (9%)
  local copies, waits for them, and re-layouts  8.05 us (4%)
    all_to_all x4, waiting for transfers between devices, exchanged(): x = lax.all_to_all(x, ('y', 'x'), split_axis=0, concat_axis=0, tiled=True)  76.9 us
    all_to_all x4, starting transfers between devices, exchanged(): x = lax.all_to_all(x, ('y', 'x'), split_axis=0, concat_axis=0, tiled=True)  31.1 us
    all_to_all x1, blocking collectives, layer(): lax.all_to_all(pieces, ('grp', 'zl'), split_axis=0, concat_axis=0, tiled=...  23 us
    dot_general x8, matrix products, dot(): return jnp.dot(a, b, preferred_element_type=F32)  15.9 us
    pallas_call x4, Pallas kernels, down(): pl.pallas_call(down_body if term is None else down_add_body, out_shape=ja...  9.26 us
    pallas_call x2, Pallas kernels, place(): pl.pallas_call(place_body, out_shape=jax.ShapeDtypeStruct((rows, width),...  8.03 us
    unnamed x20, local copies, waits for them, and re-layouts  7.2 us
    ppermute x2, waiting for transfers between devices, other_plane(): return lax.ppermute(x, 'zl', [(0, 1), (1, 0)])  5 us
  transfers between devices with their start and end apart: 10, of which 5 were waited for; matrix products, arithmetic and copies ran while one was open for 10% of the time, Pallas kernels for 8%

profile of v4, /device:TPU:2, one launch (start us, length us, event | category | flops | bytes accessed | tf_op | source)
XLA Modules:
  0.0 186.1 jit_solution(6143119451245962203)
XLA Ops:
  0.0 4.0 %place.3 = bf16[256,3584]{1,0:T(8,128)(2,1)} custom-call(s32[1]{0:T(128)} %bitcast.plane, s32[8,32]{1,0:T(8,128)} %bitcast.106, bf16[32,3584]{1,0:T(8,128)(2,1)} %tokens.1), custom_call_target="tpu_custom_call" | custom-call | tf_op jit(solution)/shard_map/place/pallas_call | solution.py:60
  4.0 7.6 %all-to-all-start.2 = ((bf16[16,16,3584]{2,1,0:T(8,128)(2,1)}), bf16[16,16,3584]{2,1,0:T(8,128)(2,1)S(1)}, u32[]{:S(2)}, u32[]{:S(2)}) async-start(bf16[16,16,3584]{2,1,0:T(8,128)(2,1)} %bitcast.95), calls=%async_computation.2 | async-start | bytes 3670016 | tf_op jit(solution)/shard_map/all_to_all | solution.py:187
  11.7 2.0 %collective-permute-start.1 = (bf16[32,3584]{1,0:T(8,128)(2,1)S(1)}, bf16[32,3584]{1,0:T(8,128)(2,1)S(1)}, u32[]{:S(2)}, u32[]{:S(2)}) collective-permute-start(bf16[32,3584]{1,0:T(8,128)(2,1)S(1)} %copy-done.6), channel_id=1, source_target_pairs={{0,2},{2,0},{1,3},{3,1},{4,6},{6,4},{5,7},{7,5},{8,10},{10,8},{9,1... | collective-permute-start | bytes 688136 | tf_op jit(solution)/shard_map/ppermute | solution.py:182
  13.7 0.2 collective-permute-start
  13.9 5.0 %collective-permute-done = f32[32,16]{0,1:T(8,128)S(1)} collective-permute-done((f32[32,16]{0,1:T(8,128)S(1)}, f32[32,16]{0,1:T(8,128)S(1)}, u32[]{:S(2)}, u32[]{:S(2)}) %collective-permute-start) | collective-permute-done | bytes 2080 | tf_op jit(solution)/shard_map/ppermute | solution.py:182
  18.9 0.6 fusion.64
  19.5 0.7 copy-done.7
  20.2 4.0 %place.2 = bf16[256,3584]{1,0:T(8,128)(2,1)} custom-call(s32[1]{0:T(128)} %bitcast.plane, s32[8,32]{1,0:T(8,128)} %get-tuple-element.21.ids_t, bf16[32,3584]{1,0:T(8,128)(2,1)} %copy-done.7), custom_call_target="tpu_custom_call" | custom-call | tf_op jit(solution)/shard_map/place/pallas_call | solution.py:60
  24.2 11.8 %all-to-all-done.2 = bf16[16,16,3584]{2,1,0:T(8,128)(2,1)S(1)} async-done(((bf16[16,16,3584]{2,1,0:T(8,128)(2,1)}), bf16[16,16,3584]{2,1,0:T(8,128)(2,1)S(1)}, u32[]{:S(2)}, u32[]{:S(2)}) %all-to-all-start.2) | async-done | bytes 1835040 | tf_op jit(solution)/shard_map/all_to_all | solution.py:187
  36.0 8.0 %all-to-all-start = ((bf16[16,16,3584]{2,1,0:T(8,128)(2,1)}), bf16[16,16,3584]{2,1,0:T(8,128)(2,1)}, u32[]{:S(2)}, u32[]{:S(2)}) async-start(bf16[16,16,3584]{2,1,0:T(8,128)(2,1)} %bitcast.96), calls=%async_computation | async-start | bytes 3670016 | tf_op jit(solution)/shard_map/all_to_all | solution.py:187
  44.0 23.4 %all-to-all-done = bf16[16,16,3584]{2,1,0:T(8,128)(2,1)} async-done(((bf16[16,16,3584]{2,1,0:T(8,128)(2,1)}), bf16[16,16,3584]{2,1,0:T(8,128)(2,1)}, u32[]{:S(2)}, u32[]{:S(2)}) %all-to-all-start) | async-done | bytes 1835040 | tf_op jit(solution)/shard_map/all_to_all | solution.py:187
  67.4 2.3 %fusion.12 = f32[256,256]{1,0:T(8,128)S(1)} fusion(bf16[256,3584]{1,0:T(8,128)(2,1)S(1)} %bitcast.89, bf16[2,3584,256]{2,1,0:T(8,128)(2,1)} %bitcast.91, s32[]{:T(128)S(6)} %select_n.84), kind=kOutput, calls=%fused_computation.12 | convolution fusion | flops 469762048 | bytes 3932164 | tf_op jit(solution)/shard_map/dot_general | solution.py:19
  69.7 0.3 copy-done.5
  69.9 0.6 fusion.4
  70.6 1.4 copy-done.4
  72.0 2.1 %fusion.27 = f32[256,256]{1,0:T(8,128)S(1)} fusion(f32[256,256]{1,0:T(8,128)S(1)} %fusion.12, bf16[256,3584]{1,0:T(8,128)(2,1)} %collective-permute-done.4, bf16[2,3584,256]{2,1,0:T(8,128)(2,1)S(1)} %bitcast.92, s32[]{:T(128)S(6)} %select_n.85), kind=kOutput, calls=%fused_computation.25 | convolution fusion | flops 469827584 | bytes 4194308 | tf_op jit(solution)/shard_map/dot_general | solution.py:19
  74.1 2.3 %multiply_convert_fusion.hidden = bf16[256,256]{1,0:T(8,128)(2,1)S(1)} fusion(f32[256,256]{1,0:T(8,128)S(1)} %fusion.27, f32[256,256]{1,0:T(8,128)S(1)} %fusion.4, bf16[256,3584]{1,0:T(8,128)(2,1)} %collective-permute-done.4, bf16[2,3584,256]{2,1,0:T(8,128)(2,1)S(1)} %bitcast.98, s32[]{:T(128)S(6)} %select_n.85), kind=kOutput, calls=%fused_computation.32 | convolution fusion | flops 470220800 | bytes 4325380 | tf_op jit(solution)/shard_map/dot_general | solution.py:19
  76.4 0.3 copy-done
  76.7 1.6 down.3
  78.3 0.6 collective-permute-start.5
  78.9 2.1 %fusion.10 = f32[256,256]{1,0:T(8,128)S(1)} fusion(bf16[256,3584]{1,0:T(8,128)(2,1)} %collective-permute-done.2, bf16[2,3584,256]{2,1,0:T(8,128)(2,1)S(1)} %bitcast.93, s32[]{:T(128)S(6)} %select_n.85), kind=kOutput, calls=%fused_computation.10 | convolution fusion | flops 469762048 | bytes 3932164 | tf_op jit(solution)/shard_map/dot_general | solution.py:19
  81.0 2.1 %fusion.2 = f32[256,256]{1,0:T(8,128)S(1)} fusion(bf16[256,3584]{1,0:T(8,128)(2,1)} %collective-permute-done.2, bf16[2,3584,256]{2,1,0:T(8,128)(2,1)S(1)} %bitcast.99, s32[]{:T(128)S(6)} %select_n.85), kind=kOutput, calls=%fused_computation.2 | convolution fusion | flops 469762048 | bytes 3932164 | tf_op jit(solution)/shard_map/dot_general | solution.py:19
  83.2 2.1 %fusion.24 = f32[256,256]{1,0:T(8,128)S(1)} fusion(f32[256,256]{1,0:T(8,128)S(1)} %fusion.10, bf16[256,3584]{1,0:T(8,128)(2,1)} %bitcast.9, bf16[2,3584,256]{2,1,0:T(8,128)(2,1)S(1)} %bitcast.94, s32[]{:T(128)S(6)} %select_n.84), kind=kOutput, calls=%fused_computation.24 | convolution fusion | flops 469827584 | bytes 4194308 | tf_op jit(solution)/shard_map/dot_general | solution.py:19
  85.3 2.1 %fusion.39.hidden = bf16[256,256]{1,0:T(8,128)(2,1)S(1)} fusion(f32[256,256]{1,0:T(8,128)S(1)} %fusion.2, bf16[256,3584]{1,0:T(8,128)(2,1)} %bitcast.9, bf16[2,3584,256]{2,1,0:T(8,128)(2,1)S(1)} %bitcast.100, s32[]{:T(128)S(6)} %select_n.84, f32[256,256]{1,0:T(8,128)S(1)} %fusion.24), kind=kOutput, calls=%fused_computation.29 | convolution fusion | flops 470220800 | bytes 4325380 | tf_op jit(solution)/shard_map/dot_general | solution.py:19
  87.5 2.7 %down.2 = bf16[256,3584]{1,0:T(8,128)(2,1)} custom-call(s32[1]{0:T(128)S(6)} %sub.46.t, bf16[256,256]{1,0:T(8,128)(2,1)S(1)} %fusion.39.hidden, bf16[256,7168]{1,0:T(8,128)(2,1)S(1)} %bitcast.81), custom_call_target="tpu_custom_call" | custom-call | tf_op jit(solution)/shard_map/down/pallas_call | solution.py:154
  90.2 1.7 down_add.3
  92.0 1.3 copy-done.3
  93.3 6.5 %all-to-all-start.3 = ((bf16[16,16,3584]{2,1,0:T(8,128)(2,1)}), bf16[16,16,3584]{2,1,0:T(8,128)(2,1)S(1)}, u32[]{:S(2)}, u32[]{:S(2)}) async-start(bf16[16,16,3584]{2,1,0:T(8,128)(2,1)} %bitcast.86), calls=%async_computation.3 | async-start | bytes 3670016 | tf_op jit(solution)/shard_map/all_to_all | solution.py:187
  99.8 0.1 broadcast_compare_fusion
  99.8 2.0 %copy-done.1 = bf16[1,256,7168]{2,1,0:T(8,128)(2,1)S(1)} copy-done((bf16[1,256,7168]{2,1,0:T(8,128)(2,1)S(1)}, bf16[1,256,7168]{2,1,0:T(8,128)(2,1)}, u32[]{:S(2)}) %copy-start.1) | copy-done | bytes 3670040
  101.9 3.2 %down_add.2 = bf16[256,3584]{1,0:T(8,128)(2,1)S(1)} custom-call(s32[1]{0:T(128)} %bitcast.6.t, bf16[256,256]{1,0:T(8,128)(2,1)S(1)} %fusion.39.hidden, bf16[256,7168]{1,0:T(8,128)(2,1)S(1)} %bitcast.83, bf16[256,3584]{1,0:T(8,128)(2,1)} %collective-permute-done.3.term), custom_call_target="tpu_custom_call" | custom-call | tf_op jit(solution)/shard_map/down_add/pallas_call | solution.py:154
  105.1 1.2 copy-done.2
  106.4 19.7 %all-to-all-done.3 = bf16[16,16,3584]{2,1,0:T(8,128)(2,1)S(1)} async-done(((bf16[16,16,3584]{2,1,0:T(8,128)(2,1)}), bf16[16,16,3584]{2,1,0:T(8,128)(2,1)S(1)}, u32[]{:S(2)}, u32[]{:S(2)}) %all-to-all-start.3) | async-done | bytes 1835040 | tf_op jit(solution)/shard_map/all_to_all | solution.py:187
  126.0 9.1 %all-to-all-start.1 = ((bf16[16,16,3584]{2,1,0:T(8,128)(2,1)}), bf16[16,16,3584]{2,1,0:T(8,128)(2,1)}, u32[]{:S(2)}, u32[]{:S(2)}) async-start(bf16[16,16,3584]{2,1,0:T(8,128)(2,1)} %bitcast.85), calls=%async_computation.1 | async-start | bytes 3670016 | tf_op jit(solution)/shard_map/all_to_all | solution.py:187
  135.1 0.1 copy.28
  135.2 0.1 eq.107
  135.3 0.1 fusion.44
  135.4 0.1 reshape.211
  135.5 0.1 convolution_bitcast_fusion.1
  135.6 0.1 reshape.212
  135.7 0.1 reshape.220
  135.8 0.1 convolution_bitcast_fusion
  135.9 0.1 reshape.221
  136.5 1.1 mix.2.first
  137.6 22.1 %all-to-all-done.1 = bf16[16,16,3584]{2,1,0:T(8,128)(2,1)} async-done(((bf16[16,16,3584]{2,1,0:T(8,128)(2,1)}), bf16[16,16,3584]{2,1,0:T(8,128)(2,1)}, u32[]{:S(2)}, u32[]{:S(2)}) %all-to-all-start.1) | async-done | bytes 1835040 | tf_op jit(solution)/shard_map/all_to_all | solution.py:187
  159.7 2.8 %mix.3 = bf16[4,2,32,896]{3,2,1,0:T(8,128)(2,1)S(1)} custom-call(s32[1]{0:T(128)} %bitcast.plane, bf16[96,256]{1,0:T(8,128)(2,1)S(1)} %pad_maximum_fusion.mix, bf16[256,3584]{1,0:T(8,128)(2,1)} %bitcast.18.rows, bf16[4,32,896]{2,1,0:T(8,128)(2,1)S(1)} %mix.2.first), custom_call_target="tpu_custom_call" | custom-call | tf_op jit(solution)/shard_map/mix/pallas_call | solution.py:126
  162.5 23.0 %all_to_all.25 = bf16[8,32,896]{2,1,0:T(8,128)(2,1)S(1)} all-to-all(bf16[8,32,896]{2,1,0:T(8,128)(2,1)S(1)} %bitcast.87), channel_id=1, replica_groups=mesh['grp'=4,'y'=4,'x'=4,'zl'=2,'tp'=2] {'grp','zl'}, dimensions={0} | all-to-all | bytes 917504 | tf_op jit(solution)/shard_map/all_to_all | solution.py:210
  185.4 0.7 reduce_sum.52
  (44 shorter events, 0.5 us)
Async XLA Ops:
  4.0 7.6 %copy-start.6 = (bf16[32,3584]{1,0:T(8,128)(2,1)S(1)}, bf16[32,3584]{1,0:T(8,128)(2,1)}, u32[]{:S(2)}) copy-start(bf16[32,3584]{1,0:T(8,128)(2,1)} %tokens.1) | copy-start | bytes 688132
  4.0 9.6 %copy-start.8 = (s32[32,8]{0,1:T(8,128)S(1)}, s32[32,8]{0,1:T(8,128)}, u32[]{:S(2)}) copy-start(s32[32,8]{0,1:T(8,128)} %param.8) | copy-start | bytes 3076
  4.0 9.6 %copy-start.9 = (f32[32,8]{0,1:T(8,128)S(1)}, f32[32,8]{0,1:T(8,128)}, u32[]{:S(2)}) copy-start(f32[32,8]{0,1:T(8,128)} %param.7) | copy-start | bytes 3076
  4.0 31.9 %all-to-all-start.2 = ((bf16[16,16,3584]{2,1,0:T(8,128)(2,1)}), bf16[16,16,3584]{2,1,0:T(8,128)(2,1)S(1)}, u32[]{:S(2)}, u32[]{:S(2)}) async-start(bf16[16,16,3584]{2,1,0:T(8,128)(2,1)} %bitcast.95), calls=%async_computation.2 | async-start | bytes 3670016 | tf_op jit(solution)/shard_map/all_to_all | solution.py:187
  11.7 7.8 %collective-permute-start.1 = (bf16[32,3584]{1,0:T(8,128)(2,1)S(1)}, bf16[32,3584]{1,0:T(8,128)(2,1)S(1)}, u32[]{:S(2)}, u32[]{:S(2)}) collective-permute-start(bf16[32,3584]{1,0:T(8,128)(2,1)S(1)} %copy-done.6), channel_id=1, source_target_pairs={{0,2},{2,0},{1,3},{3,1},{4,6},{6,4},{5,7},{7,5},{8,10},{10,8},{9,1... | collective-permute-start | bytes 688136 | tf_op jit(solution)/shard_map/ppermute | solution.py:182
  13.7 5.2 %collective-permute-start = (f32[32,16]{0,1:T(8,128)S(1)}, f32[32,16]{0,1:T(8,128)S(1)}, u32[]{:S(2)}, u32[]{:S(2)}) collective-permute-start(f32[32,16]{0,1:T(8,128)S(1)} %pad_maximum_fusion.2), channel_id=1, source_target_pairs={{0,2},{2,0},{1,3},{3,1},{4,6},{6,4},{5,7},{7,5},{8,10},{10,8},{9,1... | collective-permute-start | bytes 6152 | tf_op jit(solution)/shard_map/ppermute | solution.py:182
  19.5 0.7 copy-start.7
  36.0 31.4 %all-to-all-start = ((bf16[16,16,3584]{2,1,0:T(8,128)(2,1)}), bf16[16,16,3584]{2,1,0:T(8,128)(2,1)}, u32[]{:S(2)}, u32[]{:S(2)}) async-start(bf16[16,16,3584]{2,1,0:T(8,128)(2,1)} %bitcast.96), calls=%async_computation | async-start | bytes 3670016 | tf_op jit(solution)/shard_map/all_to_all | solution.py:187
  44.0 26.6 %collective-permute-start.4 = (bf16[256,3584]{1,0:T(8,128)(2,1)S(1)}, bf16[256,3584]{1,0:T(8,128)(2,1)}, u32[]{:S(2)}, u32[]{:S(2)}) collective-permute-start(bf16[256,3584]{1,0:T(8,128)(2,1)S(1)} %bitcast.88), channel_id=1, source_target_pairs={{0,1},{1,0},{2,3},{3,2},{4,5},{5,4},{6,7},{7,6},{8,9},{9,8},{10,11... | collective-permute-start | bytes 5505032 | tf_op jit(solution)/shard_map/ppermute | solution.py:23
  67.4 11.5 %collective-permute-start.2 = (bf16[256,3584]{1,0:T(8,128)(2,1)}, bf16[256,3584]{1,0:T(8,128)(2,1)}, u32[]{:S(2)}, u32[]{:S(2)}) collective-permute-start(bf16[256,3584]{1,0:T(8,128)(2,1)} %bitcast.9), channel_id=1, source_target_pairs={{0,1},{1,0},{2,3},{3,2},{4,5},{5,4},{6,7},{7,6},{8,9},{9,8},{10,11... | collective-permute-start | bytes 5505032 | tf_op jit(solution)/shard_map/ppermute | solution.py:23
  67.4 2.6 %copy-start.5 = (bf16[1,7168,256]{2,1,0:T(8,128)(2,1)S(1)}, bf16[1,7168,256]{2,1,0:T(8,128)(2,1)}, u32[]{:S(2)}) copy-start(bf16[1,7168,256]{2,1,0:T(8,128)(2,1)} %param.10) | copy-start | bytes 11010052
  69.9 2.0 %copy-start.4 = (bf16[1,7168,256]{2,1,0:T(8,128)(2,1)S(1)}, bf16[1,7168,256]{2,1,0:T(8,128)(2,1)}, u32[]{:S(2)}) copy-start(bf16[1,7168,256]{2,1,0:T(8,128)(2,1)} %param.9) | copy-start | bytes 11010052
  74.1 2.6 %copy-start = (bf16[1,256,7168]{2,1,0:T(8,128)(2,1)S(1)}, bf16[1,256,7168]{2,1,0:T(8,128)(2,1)}, u32[]{:S(2)}) copy-start(bf16[1,256,7168]{2,1,0:T(8,128)(2,1)} %param.11) | copy-start | bytes 11010052
  78.3 11.9 %collective-permute-start.5 = (bf16[256,3584]{1,0:T(8,128)(2,1)S(1)}, bf16[256,3584]{1,0:T(8,128)(2,1)S(1)}, u32[]{:S(2)}, u32[]{:S(2)}) collective-permute-start(bf16[256,3584]{1,0:T(8,128)(2,1)S(1)} %down.3), channel_id=1, source_target_pairs={{0,1},{1,0},{2,3},{3,2},{4,5},{5,4},{6,7},{7,6},{8,9},{9,8},{10,11... | collective-permute-start | bytes 5505032 | tf_op jit(solution)/shard_map/ppermute | solution.py:23
  90.2 9.6 %collective-permute-start.3 = (bf16[256,3584]{1,0:T(8,128)(2,1)}, bf16[256,3584]{1,0:T(8,128)(2,1)}, u32[]{:S(2)}, u32[]{:S(2)}) collective-permute-start(bf16[256,3584]{1,0:T(8,128)(2,1)} %down.2), channel_id=1, source_target_pairs={{0,1},{1,0},{2,3},{3,2},{4,5},{5,4},{6,7},{7,6},{8,9},{9,8},{10,11... | collective-permute-start | bytes 5505032 | tf_op jit(solution)/shard_map/ppermute | solution.py:23
  92.0 1.3 copy-start.3
  93.3 32.8 %all-to-all-start.3 = ((bf16[16,16,3584]{2,1,0:T(8,128)(2,1)}), bf16[16,16,3584]{2,1,0:T(8,128)(2,1)S(1)}, u32[]{:S(2)}, u32[]{:S(2)}) async-start(bf16[16,16,3584]{2,1,0:T(8,128)(2,1)} %bitcast.86), calls=%async_computation.3 | async-start | bytes 3670016 | tf_op jit(solution)/shard_map/all_to_all | solution.py:187
  99.8 2.0 %copy-start.1 = (bf16[1,256,7168]{2,1,0:T(8,128)(2,1)S(1)}, bf16[1,256,7168]{2,1,0:T(8,128)(2,1)}, u32[]{:S(2)}) copy-start(bf16[1,256,7168]{2,1,0:T(8,128)(2,1)} %param.11) | copy-start | bytes 11010052
  105.1 1.2 copy-start.2
  126.0 33.6 %all-to-all-start.1 = ((bf16[16,16,3584]{2,1,0:T(8,128)(2,1)}), bf16[16,16,3584]{2,1,0:T(8,128)(2,1)}, u32[]{:S(2)}, u32[]{:S(2)}) async-start(bf16[16,16,3584]{2,1,0:T(8,128)(2,1)} %bitcast.85), calls=%async_computation.1 | async-start | bytes 3670016 | tf_op jit(solution)/shard_map/all_to_all | solution.py:187

commit v5 on v3

--- a/solution.py
+++ b/solution.py
@@ -55,11 +55,11 @@
 def place(tokens, expert_ids, micro):
     count, width = tokens.shape
     rows = EXPERTS * CAP
-    block = width // 4
+    block = width // 2
     return pl.pallas_call(
         lambda *refs: place_body(micro, *refs),
         out_shape=jax.ShapeDtypeStruct((rows, width), BF),
-        grid=(4,),
+        grid=(2,),
         in_specs=[
             pl.BlockSpec(expert_ids.shape[::-1], lambda i: (0, 0)),
             pl.BlockSpec((count, block), lambda i: (0, i)),
@@ -115,6 +115,43 @@
         interpret=INTERPRET,
         name="mix",
     )(first, mix, rows)
+
+
+def mix_last_body(mix, rows, out, acc):
+    part = dot(mix[...], rows[...])
+    step = pl.program_id(0)
+
+    @pl.when(step == 0)
+    def _():
+        acc[...] = part
+
+    @pl.when(step == pl.num_programs(0) - 1)
+    def _():
+        total = acc[...] + part
+        blocks, n, block = out.shape
+        total = (total[:n] + total[n : 2 * n] + total[2 * n :]).astype(BF)
+        for b in range(blocks):
+            out[b] = total[:, b * block : (b + 1) * block]
+
+
+def mix_last(mix, rows):
+    slots, width = rows.shape
+    count = mix.shape[0] // 3
+    half = slots // 2
+    return pl.pallas_call(
+        mix_last_body,
+        out_shape=jax.ShapeDtypeStruct((4, count, width // 4), BF),
+        grid=(2,),
+        in_specs=[
+            pl.BlockSpec((mix.shape[0], half), lambda i: (0, i)),
+            pl.BlockSpec((half, width), lambda i: (i, 0)),
+        ],
+        out_specs=pl.BlockSpec((4, count, width // 4), lambda i: (0, 0, 0)),
+        scratch_shapes=[pltpu.VMEM((mix.shape[0], width), F32)],
+        compiler_params=pltpu.CompilerParams(vmem_limit_bytes=8 << 20),
+        interpret=INTERPRET,
+        name="mix_last",
+    )(mix, rows)
 
 
 def down_body(t, hidden, weight, out):
@@ -186,7 +223,7 @@
                 ring = [(i, (i + d) % 4) for i in range(4)]
                 total += lax.ppermute(blocks[d], "grp", ring).astype(F32)
         else:
-            blocks = mix_rows(mix, back, jnp.zeros_like(group))
+            blocks = mix_last(mix, back)
             shares = lax.all_to_all(blocks, "grp", split_axis=0, concat_axis=0, tiled=True)
             total = jnp.sum(shares.astype(F32), axis=0)
         results.append(total.astype(BF))

time: 166 us -> 163 us (0.982)
  Pallas kernels: 23.5 us -> 20.1 us
    pallas_call x2 -> x1, Pallas kernels: 4.76 us -> 1.07 us  [mix_rows(): pl.pallas_call(mix_body, out_shape=jax.ShapeDtypeStruct((4, count, block)...]
    pallas_call x0 -> x1, Pallas kernels: none -> 2.46 us  [mix_last(): pl.pallas_call(mix_last_body, out_shape=jax.ShapeDtypeStruct((4, count, w...]
    pallas_call x2, Pallas kernels: 8.07 us -> 5.86 us  [place(): pl.pallas_call(lambda *refs: place_body(micro, *refs), out_shape=jax.Shap...]
  transfers between devices with their start and end apart: 12 -> 12, of which waited for: 6 -> 6; matrix products, arithmetic and copies ran while one was open for 11% -> 12% of each run, Pallas kernels for 12% -> 11%
where the time goes in v5:
time: 163 us; the launch traced here: 162 us
  waiting for transfers between devices  66.8 us (41%)
  starting transfers between devices  45.8 us (28%)
  Pallas kernels  20.1 us (12%)
  matrix products  17.2 us (11%)
  local copies, waits for them, and re-layouts  10.6 us (7%)
    all_to_all x4, waiting for transfers between devices, exchanged(): x = lax.all_to_all(x, 'ep', split_axis=0, concat_axis=0, tiled=True)  54.6 us
    all_to_all x4, starting transfers between devices, exchanged(): x = lax.all_to_all(x, 'ep', split_axis=0, concat_axis=0, tiled=True)  27.1 us
    dot_general x8, matrix products, dot(): return jnp.dot(a, b, preferred_element_type=F32)  16.9 us
    pallas_call x4, Pallas kernels, down(): pl.pallas_call(down_body if term is None else down_add_body, out_shape=ja...  10.7 us
    ppermute x3, starting transfers between devices, layer(): total += lax.ppermute(blocks[d], 'grp', ring).astype(F32)  10.5 us
    unnamed x24, local copies, waits for them, and re-layouts  9.36 us
    all_to_all x1, waiting for transfers between devices, layer(): lax.all_to_all(blocks, 'grp', split_axis=0, concat_axis=0, tiled=True)  8.24 us
    all_to_all x1, starting transfers between devices, layer(): lax.all_to_all(blocks, 'grp', split_axis=0, concat_axis=0, tiled=True)  7.85 us
  transfers between devices with their start and end apart: 12, of which 6 were waited for; matrix products, arithmetic and copies ran while one was open for 12% of the time, Pallas kernels for 11%

profile of v5, /device:TPU:2, one launch (start us, length us, event | category | flops | bytes accessed | tf_op | source)
XLA Modules:
  0.0 161.8 jit_solution(7649250311191944940)
XLA Ops:
  0.0 2.9 %place.2 = bf16[256,3584]{1,0:T(8,128)(2,1)} custom-call(s32[8,32]{1,0:T(8,128)} %bitcast.115, bf16[32,3584]{1,0:T(8,128)(2,1)} %refs_1_.3), custom_call_target="tpu_custom_call" | custom-call | tf_op jit(solution)/shard_map/place/pallas_call | solution.py:59
  2.9 9.0 %all-to-all-start = ((bf16[32,8,3584]{2,1,0:T(8,128)(2,1)}), bf16[32,8,3584]{2,1,0:T(8,128)(2,1)S(1)}, u32[]{:S(2)}, u32[]{:S(2)}) async-start(bf16[32,8,3584]{2,1,0:T(8,128)(2,1)} %bitcast.110), calls=%async_computation | async-start | bytes 3670016 | tf_op jit(solution)/shard_map/all_to_all | solution.py:203
  11.9 3.0 %place.3 = bf16[256,3584]{1,0:T(8,128)(2,1)} custom-call(s32[8,32]{1,0:T(8,128)} %bitcast.116, bf16[32,3584]{1,0:T(8,128)(2,1)} %refs_1_.3), custom_call_target="tpu_custom_call" | custom-call | tf_op jit(solution)/shard_map/place/pallas_call | solution.py:59
  14.8 22.4 %all-to-all-done = bf16[32,8,3584]{2,1,0:T(8,128)(2,1)S(1)} async-done(((bf16[32,8,3584]{2,1,0:T(8,128)(2,1)}), bf16[32,8,3584]{2,1,0:T(8,128)(2,1)S(1)}, u32[]{:S(2)}, u32[]{:S(2)}) %all-to-all-start) | async-done | bytes 1835040 | tf_op jit(solution)/shard_map/all_to_all | solution.py:203
  37.2 5.7 %all-to-all-start.2 = ((bf16[32,8,3584]{2,1,0:T(8,128)(2,1)}), bf16[32,8,3584]{2,1,0:T(8,128)(2,1)}, u32[]{:S(2)}, u32[]{:S(2)}) async-start(bf16[32,8,3584]{2,1,0:T(8,128)(2,1)} %bitcast.109), calls=%async_computation.2 | async-start | bytes 3670016 | tf_op jit(solution)/shard_map/all_to_all | solution.py:203
  43.0 2.3 %fusion.14 = f32[256,256]{1,0:T(8,128)S(1)} fusion(bf16[2,3584,256]{2,1,0:T(8,128)(2,1)} %bitcast.105, s32[]{:T(128)S(6)} %select_n.84, bf16[32,8,3584]{2,1,0:T(8,128)(2,1)S(1)} %all-to-all-done), kind=kOutput, calls=%fused_computation.14 | convolution fusion | flops 469762048 | bytes 3932164 | tf_op jit(solution)/shard_map/dot_general | solution.py:19
  45.3 0.3 copy-done.8
  45.6 0.6 fusion.6
  46.2 1.4 copy-done.6
  47.6 2.1 %fusion.24 = f32[256,256]{1,0:T(8,128)S(1)} fusion(f32[256,256]{1,0:T(8,128)S(1)} %fusion.14, bf16[256,3584]{1,0:T(8,128)(2,1)} %collective-permute-done, bf16[2,3584,256]{2,1,0:T(8,128)(2,1)S(1)} %bitcast.107, s32[]{:T(128)S(6)} %select_n.85), kind=kOutput, calls=%fused_computation.24 | convolution fusion | flops 469827584 | bytes 4194308 | tf_op jit(solution)/shard_map/dot_general | solution.py:19
  49.8 2.3 %multiply_convert_fusion.1.hidden = bf16[256,256]{1,0:T(8,128)(2,1)S(1)} fusion(f32[256,256]{1,0:T(8,128)S(1)} %fusion.24, f32[256,256]{1,0:T(8,128)S(1)} %fusion.6, bf16[256,3584]{1,0:T(8,128)(2,1)} %collective-permute-done, bf16[2,3584,256]{2,1,0:T(8,128)(2,1)S(1)} %bitcast.112, s32[]{:T(128)S(6)} %select_n.85), kind=kOutput, calls=%fused_computation.33 | convolution fusion | flops 470220800 | bytes 4325380 | tf_op jit(solution)/shard_map/dot_general | solution.py:19
  52.1 0.3 copy-done
  52.3 1.6 down.2
  53.9 0.3 collective-permute-start.1
  54.2 16.3 %all-to-all-done.2 = bf16[32,8,3584]{2,1,0:T(8,128)(2,1)} async-done(((bf16[32,8,3584]{2,1,0:T(8,128)(2,1)}), bf16[32,8,3584]{2,1,0:T(8,128)(2,1)}, u32[]{:S(2)}, u32[]{:S(2)}) %all-to-all-start.2) | async-done | bytes 1835040 | tf_op jit(solution)/shard_map/all_to_all | solution.py:203
  70.5 2.0 %copy-done.1 = bf16[1,256,7168]{2,1,0:T(8,128)(2,1)S(1)} copy-done((bf16[1,256,7168]{2,1,0:T(8,128)(2,1)S(1)}, bf16[1,256,7168]{2,1,0:T(8,128)(2,1)}, u32[]{:S(2)}) %copy-start.1) | copy-done | bytes 3670040
  72.6 3.2 %down_add.2 = bf16[256,3584]{1,0:T(8,128)(2,1)S(1)} custom-call(s32[1]{0:T(128)} %bitcast.7.t, bf16[256,256]{1,0:T(8,128)(2,1)S(1)} %multiply_convert_fusion.1.hidden, bf16[256,7168]{1,0:T(8,128)(2,1)S(1)} %bitcast.98, bf16[256,3584]{1,0:T(8,128)(2,1)} %collective-permute-done.1.term), custom_call_target="tpu_custom_call" | custom-call | tf_op jit(solution)/shard_map/down_add/pallas_call | solution.py:173
  75.8 1.3 copy-done.5
  77.1 6.3 %all-to-all-start.1 = ((bf16[32,8,3584]{2,1,0:T(8,128)(2,1)}), bf16[32,8,3584]{2,1,0:T(8,128)(2,1)S(1)}, u32[]{:S(2)}, u32[]{:S(2)}) async-start(bf16[32,8,3584]{2,1,0:T(8,128)(2,1)} %bitcast.103), calls=%async_computation.1 | async-start | bytes 3670016 | tf_op jit(solution)/shard_map/all_to_all | solution.py:203
  83.4 2.8 %fusion.12 = f32[256,256]{1,0:T(8,128)S(1)} fusion(bf16[2,3584,256]{2,1,0:T(8,128)(2,1)} %bitcast.106, s32[]{:T(128)S(6)} %select_n.84, bf16[32,8,3584]{2,1,0:T(8,128)(2,1)} %all-to-all-done.2), kind=kOutput, calls=%fused_computation.12 | convolution fusion | flops 469762048 | bytes 3932164 | tf_op jit(solution)/shard_map/dot_general | solution.py:19
  86.2 0.3 copy-done.9
  86.5 2.3 %fusion.4 = f32[256,256]{1,0:T(8,128)S(1)} fusion(bf16[2,3584,256]{2,1,0:T(8,128)(2,1)S(1)} %bitcast.113, s32[]{:T(128)S(6)} %select_n.84, bf16[32,8,3584]{2,1,0:T(8,128)(2,1)} %all-to-all-done.2), kind=kOutput, calls=%fused_computation.4 | convolution fusion | flops 469762048 | bytes 3932164 | tf_op jit(solution)/shard_map/dot_general | solution.py:19
  88.8 0.3 copy-done.7
  89.1 2.1 %fusion.27 = f32[256,256]{1,0:T(8,128)S(1)} fusion(f32[256,256]{1,0:T(8,128)S(1)} %fusion.12, bf16[256,3584]{1,0:T(8,128)(2,1)} %collective-permute-done.5, bf16[2,3584,256]{2,1,0:T(8,128)(2,1)S(1)} %bitcast.108, s32[]{:T(128)S(6)} %select_n.85), kind=kOutput, calls=%fused_computation.25 | convolution fusion | flops 469827584 | bytes 4194308 | tf_op jit(solution)/shard_map/dot_general | solution.py:19
  91.3 2.3 %multiply_convert_fusion.hidden = bf16[256,256]{1,0:T(8,128)(2,1)S(1)} fusion(f32[256,256]{1,0:T(8,128)S(1)} %fusion.27, f32[256,256]{1,0:T(8,128)S(1)} %fusion.4, bf16[256,3584]{1,0:T(8,128)(2,1)} %collective-permute-done.5, bf16[2,3584,256]{2,1,0:T(8,128)(2,1)S(1)} %bitcast.114, s32[]{:T(128)S(6)} %select_n.85), kind=kOutput, calls=%fused_computation.32 | convolution fusion | flops 470220800 | bytes 4325380 | tf_op jit(solution)/shard_map/dot_general | solution.py:19
  93.6 0.3 copy-done.2
  93.9 2.7 %down.3 = bf16[256,3584]{1,0:T(8,128)(2,1)} custom-call(s32[1]{0:T(128)S(6)} %sub.43.t, bf16[256,256]{1,0:T(8,128)(2,1)S(1)} %multiply_convert_fusion.hidden, bf16[256,7168]{1,0:T(8,128)(2,1)S(1)} %bitcast.99), custom_call_target="tpu_custom_call" | custom-call | tf_op jit(solution)/shard_map/down/pallas_call | solution.py:173
  96.7 4.0 %collective-permute-done.6.term = bf16[256,3584]{1,0:T(8,128)(2,1)} collective-permute-done((bf16[256,3584]{1,0:T(8,128)(2,1)}, bf16[256,3584]{1,0:T(8,128)(2,1)}, u32[]{:S(2)}, u32[]{:S(2)}) %collective-permute-start.6) | collective-permute-done | bytes 1835040 | tf_op jit(solution)/shard_map/ppermute | solution.py:23
  100.6 2.0 %copy-done.3 = bf16[1,256,7168]{2,1,0:T(8,128)(2,1)S(1)} copy-done((bf16[1,256,7168]{2,1,0:T(8,128)(2,1)S(1)}, bf16[1,256,7168]{2,1,0:T(8,128)(2,1)}, u32[]{:S(2)}) %copy-start.3) | copy-done | bytes 3670040
  102.7 3.2 %down_add.3 = bf16[256,3584]{1,0:T(8,128)(2,1)S(1)} custom-call(s32[1]{0:T(128)} %bitcast.7.t, bf16[256,256]{1,0:T(8,128)(2,1)S(1)} %multiply_convert_fusion.hidden, bf16[256,7168]{1,0:T(8,128)(2,1)S(1)} %bitcast.100, bf16[256,3584]{1,0:T(8,128)(2,1)} %collective-permute-done.6.term), custom_call_target="tpu_custom_call" | custom-call | tf_op jit(solution)/shard_map/down_add/pallas_call | solution.py:173
  105.9 1.2 copy-done.4
  107.2 3.0 %all-to-all-done.1 = bf16[32,8,3584]{2,1,0:T(8,128)(2,1)S(1)} async-done(((bf16[32,8,3584]{2,1,0:T(8,128)(2,1)}), bf16[32,8,3584]{2,1,0:T(8,128)(2,1)S(1)}, u32[]{:S(2)}, u32[]{:S(2)}) %all-to-all-start.1) | async-done | bytes 1835040 | tf_op jit(solution)/shard_map/all_to_all | solution.py:203
  110.2 6.1 %all-to-all-start.3 = ((bf16[32,8,3584]{2,1,0:T(8,128)(2,1)}), bf16[32,8,3584]{2,1,0:T(8,128)(2,1)}, u32[]{:S(2)}, u32[]{:S(2)}) async-start(bf16[32,8,3584]{2,1,0:T(8,128)(2,1)} %bitcast.102), calls=%async_computation.3 | async-start | bytes 3670016 | tf_op jit(solution)/shard_map/all_to_all | solution.py:203
  116.5 0.1 convert_reduce_fusion.1
  116.6 0.1 fusion.37
  117.0 0.1 convert_reduce_fusion
  117.2 0.1 fusion.36
  117.8 0.1 broadcast_compare_fusion
  118.0 0.1 eq.109
  118.1 1.1 mix.1
  119.2 3.3 %collective-permute-start.2 = (bf16[16,896]{1,0:T(8,128)(2,1)S(1)}, bf16[16,896]{1,0:T(8,128)(2,1)S(1)}, u32[]{:S(2)}, u32[]{:S(2)}) collective-permute-start(bf16[16,896]{1,0:T(8,128)(2,1)S(1)} %get-tuple-element.13), channel_id=1, source_target_pairs={{0,64},{64,128},{128,192},{192,0},{1,65},{65,129},{129,193},{193,1... | collective-permute-start | bytes 86024 | tf_op jit(solution)/shard_map/ppermute | solution.py:224
  122.6 4.5 %collective-permute-start.3 = (bf16[16,896]{1,0:T(8,128)(2,1)S(1)}, bf16[16,896]{1,0:T(8,128)(2,1)S(1)}, u32[]{:S(2)}, u32[]{:S(2)}) collective-permute-start(bf16[16,896]{1,0:T(8,128)(2,1)S(1)} %get-tuple-element.15), channel_id=1, source_target_pairs={{0,128},{64,192},{128,0},{192,64},{1,129},{65,193},{129,1},{193,65... | collective-permute-start | bytes 86024 | tf_op jit(solution)/shard_map/ppermute | solution.py:224
  127.1 2.6 %collective-permute-start.4 = (bf16[16,896]{1,0:T(8,128)(2,1)S(1)}, bf16[16,896]{1,0:T(8,128)(2,1)S(1)}, u32[]{:S(2)}, u32[]{:S(2)}) collective-permute-start(bf16[16,896]{1,0:T(8,128)(2,1)S(1)} %get-tuple-element.14), channel_id=1, source_target_pairs={{0,192},{64,0},{128,64},{192,128},{1,193},{65,1},{129,65},{193,129... | collective-permute-start | bytes 86024 | tf_op jit(solution)/shard_map/ppermute | solution.py:224
  129.7 12.9 %all-to-all-done.3 = bf16[32,8,3584]{2,1,0:T(8,128)(2,1)} async-done(((bf16[32,8,3584]{2,1,0:T(8,128)(2,1)}), bf16[32,8,3584]{2,1,0:T(8,128)(2,1)}, u32[]{:S(2)}, u32[]{:S(2)}) %all-to-all-start.3) | async-done | bytes 1835040 | tf_op jit(solution)/shard_map/all_to_all | solution.py:203
  142.6 2.5 %mix_last.1 = bf16[4,16,896]{2,1,0:T(8,128)(2,1)} custom-call(bf16[48,256]{1,0:T(8,128)(2,1)S(1)} %pad_maximum_fusion.2.mix, bf16[256,3584]{1,0:T(8,128)(2,1)} %bitcast.32.rows), custom_call_target="tpu_custom_call" | custom-call | tf_op jit(solution)/shard_map/mix_last/pallas_call | solution.py:141
  145.0 7.8 %all-to-all-start.4 = ((bf16[4,16,896]{2,1,0:T(8,128)(2,1)}), bf16[4,16,896]{2,1,0:T(8,128)(2,1)S(1)}, u32[]{:S(2)}, u32[]{:S(2)}) async-start(bf16[4,16,896]{2,1,0:T(8,128)(2,1)} %mix_last.1), calls=%async_computation.4 | async-start | bytes 229376 | tf_op jit(solution)/shard_map/all_to_all | solution.py:227
  152.9 8.2 %all-to-all-done.4 = bf16[4,16,896]{2,1,0:T(8,128)(2,1)S(1)} async-done(((bf16[4,16,896]{2,1,0:T(8,128)(2,1)}), bf16[4,16,896]{2,1,0:T(8,128)(2,1)S(1)}, u32[]{:S(2)}, u32[]{:S(2)}) %all-to-all-start.4) | async-done | bytes 114720 | tf_op jit(solution)/shard_map/all_to_all | solution.py:227
  161.2 0.6 pad_maximum_fusion
  (54 shorter events, 1.3 us)
Async XLA Ops:
  2.9 34.3 %all-to-all-start = ((bf16[32,8,3584]{2,1,0:T(8,128)(2,1)}), bf16[32,8,3584]{2,1,0:T(8,128)(2,1)S(1)}, u32[]{:S(2)}, u32[]{:S(2)}) async-start(bf16[32,8,3584]{2,1,0:T(8,128)(2,1)} %bitcast.110), calls=%async_computation | async-start | bytes 3670016 | tf_op jit(solution)/shard_map/all_to_all | solution.py:203
  37.2 9.0 %collective-permute-start = (bf16[256,3584]{1,0:T(8,128)(2,1)S(1)}, bf16[256,3584]{1,0:T(8,128)(2,1)}, u32[]{:S(2)}, u32[]{:S(2)}) collective-permute-start(bf16[256,3584]{1,0:T(8,128)(2,1)S(1)} %bitcast.104), channel_id=1, source_target_pairs={{0,1},{1,0},{2,3},{3,2},{4,5},{5,4},{6,7},{7,6},{8,9},{9,8},{10,11... | collective-permute-start | bytes 5505032 | tf_op jit(solution)/shard_map/ppermute | solution.py:23
  37.2 33.3 %all-to-all-start.2 = ((bf16[32,8,3584]{2,1,0:T(8,128)(2,1)}), bf16[32,8,3584]{2,1,0:T(8,128)(2,1)}, u32[]{:S(2)}, u32[]{:S(2)}) async-start(bf16[32,8,3584]{2,1,0:T(8,128)(2,1)} %bitcast.109), calls=%async_computation.2 | async-start | bytes 3670016 | tf_op jit(solution)/shard_map/all_to_all | solution.py:203
  43.0 2.6 %copy-start.8 = (bf16[1,7168,256]{2,1,0:T(8,128)(2,1)S(1)}, bf16[1,7168,256]{2,1,0:T(8,128)(2,1)}, u32[]{:S(2)}) copy-start(bf16[1,7168,256]{2,1,0:T(8,128)(2,1)} %param.10) | copy-start | bytes 11010052
  45.6 2.0 %copy-start.6 = (bf16[1,7168,256]{2,1,0:T(8,128)(2,1)S(1)}, bf16[1,7168,256]{2,1,0:T(8,128)(2,1)}, u32[]{:S(2)}) copy-start(bf16[1,7168,256]{2,1,0:T(8,128)(2,1)} %param.9) | copy-start | bytes 11010052
  49.8 2.6 %copy-start = (bf16[1,256,7168]{2,1,0:T(8,128)(2,1)S(1)}, bf16[1,256,7168]{2,1,0:T(8,128)(2,1)}, u32[]{:S(2)}) copy-start(bf16[1,256,7168]{2,1,0:T(8,128)(2,1)} %param.11) | copy-start | bytes 11010052
  53.9 16.6 %collective-permute-start.1 = (bf16[256,3584]{1,0:T(8,128)(2,1)S(1)}, bf16[256,3584]{1,0:T(8,128)(2,1)}, u32[]{:S(2)}, u32[]{:S(2)}) collective-permute-start(bf16[256,3584]{1,0:T(8,128)(2,1)S(1)} %down.2), channel_id=1, source_target_pairs={{0,1},{1,0},{2,3},{3,2},{4,5},{5,4},{6,7},{7,6},{8,9},{9,8},{10,11... | collective-permute-start | bytes 5505032 | tf_op jit(solution)/shard_map/ppermute | solution.py:23
  70.5 18.3 %collective-permute-start.5 = (bf16[256,3584]{1,0:T(8,128)(2,1)}, bf16[256,3584]{1,0:T(8,128)(2,1)}, u32[]{:S(2)}, u32[]{:S(2)}) collective-permute-start(bf16[256,3584]{1,0:T(8,128)(2,1)} %bitcast.30), channel_id=1, source_target_pairs={{0,1},{1,0},{2,3},{3,2},{4,5},{5,4},{6,7},{7,6},{8,9},{9,8},{10,11... | collective-permute-start | bytes 5505032 | tf_op jit(solution)/shard_map/ppermute | solution.py:23
  70.5 2.0 %copy-start.1 = (bf16[1,256,7168]{2,1,0:T(8,128)(2,1)S(1)}, bf16[1,256,7168]{2,1,0:T(8,128)(2,1)}, u32[]{:S(2)}) copy-start(bf16[1,256,7168]{2,1,0:T(8,128)(2,1)} %param.11) | copy-start | bytes 11010052
  75.8 1.3 copy-start.5
  77.1 33.1 %all-to-all-start.1 = ((bf16[32,8,3584]{2,1,0:T(8,128)(2,1)}), bf16[32,8,3584]{2,1,0:T(8,128)(2,1)S(1)}, u32[]{:S(2)}, u32[]{:S(2)}) async-start(bf16[32,8,3584]{2,1,0:T(8,128)(2,1)} %bitcast.103), calls=%async_computation.1 | async-start | bytes 3670016 | tf_op jit(solution)/shard_map/all_to_all | solution.py:203
  83.4 3.1 %copy-start.9 = (bf16[1,7168,256]{2,1,0:T(8,128)(2,1)S(1)}, bf16[1,7168,256]{2,1,0:T(8,128)(2,1)}, u32[]{:S(2)}) copy-start(bf16[1,7168,256]{2,1,0:T(8,128)(2,1)} %param.10) | copy-start | bytes 11010052
  86.5 2.6 %copy-start.7 = (bf16[1,7168,256]{2,1,0:T(8,128)(2,1)S(1)}, bf16[1,7168,256]{2,1,0:T(8,128)(2,1)}, u32[]{:S(2)}) copy-start(bf16[1,7168,256]{2,1,0:T(8,128)(2,1)} %param.9) | copy-start | bytes 11010052
  91.3 2.6 %copy-start.2 = (bf16[1,256,7168]{2,1,0:T(8,128)(2,1)S(1)}, bf16[1,256,7168]{2,1,0:T(8,128)(2,1)}, u32[]{:S(2)}) copy-start(bf16[1,256,7168]{2,1,0:T(8,128)(2,1)} %param.11) | copy-start | bytes 11010052
  93.9 2.7 %copy-start.10 = (s32[32,8]{0,1:T(8,128)S(1)}, s32[32,8]{0,1:T(8,128)}, u32[]{:S(2)}) copy-start(s32[32,8]{0,1:T(8,128)} %param.8) | copy-start | bytes 3076
  96.5 4.1 %collective-permute-start.6 = (bf16[256,3584]{1,0:T(8,128)(2,1)}, bf16[256,3584]{1,0:T(8,128)(2,1)}, u32[]{:S(2)}, u32[]{:S(2)}) collective-permute-start(bf16[256,3584]{1,0:T(8,128)(2,1)} %down.3), channel_id=1, source_target_pairs={{0,1},{1,0},{2,3},{3,2},{4,5},{5,4},{6,7},{7,6},{8,9},{9,8},{10,11... | collective-permute-start | bytes 5505032 | tf_op jit(solution)/shard_map/ppermute | solution.py:23
  100.6 2.0 %copy-start.3 = (bf16[1,256,7168]{2,1,0:T(8,128)(2,1)S(1)}, bf16[1,256,7168]{2,1,0:T(8,128)(2,1)}, u32[]{:S(2)}) copy-start(bf16[1,256,7168]{2,1,0:T(8,128)(2,1)} %param.11) | copy-start | bytes 11010052
  105.9 1.2 copy-start.4
  110.2 6.1 %copy-start.11 = (f32[32,8]{0,1:T(8,128)S(1)}, f32[32,8]{0,1:T(8,128)}, u32[]{:S(2)}) copy-start(f32[32,8]{0,1:T(8,128)} %param.7) | copy-start | bytes 3076
  110.2 32.4 %all-to-all-start.3 = ((bf16[32,8,3584]{2,1,0:T(8,128)(2,1)}), bf16[32,8,3584]{2,1,0:T(8,128)(2,1)}, u32[]{:S(2)}, u32[]{:S(2)}) async-start(bf16[32,8,3584]{2,1,0:T(8,128)(2,1)} %bitcast.102), calls=%async_computation.3 | async-start | bytes 3670016 | tf_op jit(solution)/shard_map/all_to_all | solution.py:203
  119.2 33.7 %collective-permute-start.2 = (bf16[16,896]{1,0:T(8,128)(2,1)S(1)}, bf16[16,896]{1,0:T(8,128)(2,1)S(1)}, u32[]{:S(2)}, u32[]{:S(2)}) collective-permute-start(bf16[16,896]{1,0:T(8,128)(2,1)S(1)} %get-tuple-element.13), channel_id=1, source_target_pairs={{0,64},{64,128},{128,192},{192,0},{1,65},{65,129},{129,193},{193,1... | collective-permute-start | bytes 86024 | tf_op jit(solution)/shard_map/ppermute | solution.py:224
  122.6 30.3 %collective-permute-start.3 = (bf16[16,896]{1,0:T(8,128)(2,1)S(1)}, bf16[16,896]{1,0:T(8,128)(2,1)S(1)}, u32[]{:S(2)}, u32[]{:S(2)}) collective-permute-start(bf16[16,896]{1,0:T(8,128)(2,1)S(1)} %get-tuple-element.15), channel_id=1, source_target_pairs={{0,128},{64,192},{128,0},{192,64},{1,129},{65,193},{129,1},{193,65... | collective-permute-start | bytes 86024 | tf_op jit(solution)/shard_map/ppermute | solution.py:224
  127.1 25.8 %collective-permute-start.4 = (bf16[16,896]{1,0:T(8,128)(2,1)S(1)}, bf16[16,896]{1,0:T(8,128)(2,1)S(1)}, u32[]{:S(2)}, u32[]{:S(2)}) collective-permute-start(bf16[16,896]{1,0:T(8,128)(2,1)S(1)} %get-tuple-element.14), channel_id=1, source_target_pairs={{0,192},{64,0},{128,64},{192,128},{1,193},{65,1},{129,65},{193,129... | collective-permute-start | bytes 86024 | tf_op jit(solution)/shard_map/ppermute | solution.py:224
  145.0 16.1 %all-to-all-start.4 = ((bf16[4,16,896]{2,1,0:T(8,128)(2,1)}), bf16[4,16,896]{2,1,0:T(8,128)(2,1)S(1)}, u32[]{:S(2)}, u32[]{:S(2)}) async-start(bf16[4,16,896]{2,1,0:T(8,128)(2,1)} %mix_last.1), calls=%async_computation.4 | async-start | bytes 229376 | tf_op jit(solution)/shard_map/all_to_all | solution.py:227
